TPU v7x, 256 devices: a whole 4x4x8 slice. The times are simulated.
256 devices in a mesh: gx: 8 (over z), gy: 16 (over y_hi, x, core), ens: 2 (over y_lo).
Axes of the slice: x: 4, y: 4 (y_hi: 2, y_lo: 2; y = y_hi * 2 + y_lo), z: 8, core: 2. Of those that a mesh axis runs over, the one named last changes fastest.
Arguments:
- state: float32 [128, 256, 1024], P('ens', 'gy', 'gx'), may hold values from -6 to 6
- u_vel: float32 [256, 1024], P('gy', 'gx'), may hold values from -0.4 to 0.4
- v_vel: float32 [256, 1024], P('gy', 'gx'), may hold values from -0.4 to 0.4
- land: int32 [256, 1024], P('gy', 'gx'), may hold values 0 or 1
- forcing: float32 [8, 256, 1024], P(None, 'gy', 'gx'), may hold values from -3 to 3
- member_mode: int32 [128], P('ens'), may hold values from 0 to 7
- theta: float32 [128, 4], P('ens'), may hold values from -1 to 1
- obs_index: int32 [16, 8, 128], P('gy', 'gx'), may hold values from 0 to 2047
- obs_values: float32 [16, 8, 128], P('gy', 'gx'), may hold values from -6 to 6
- obs_sigma: float32 [16, 8, 128], P('gy', 'gx'), may hold values from 0.5 to 4
Outputs:
- final_state: float32 [128, 256, 1024], P('ens', 'gy', 'gx')
- new_theta: float32 [128, 4], P('ens')
All inputs are finite; a program needn't handle non-finite values. No bound on the sum of `land` on one device may be relied on, other than what follows from the above.
Results may differ from a plain program's by a relative error of at most 0.0003.
Values sent between devices are 32-bit elements; how exact they have to be, the bound alone decides.
A program may use at most 64 MiB of HBM per device.

v0:
```python
import jax
import jax.numpy as jnp
from jax import lax
from jax.sharding import Mesh
from jax.sharding import PartitionSpec as P

STEPS = 4
GY = ("gy_0", "gy_1", "gy_2")


def with_halo(block, sides, width):
    for axis, dim in sides:
        count = lax.axis_size(axis)
        forward = [(i, i + 1) for i in range(count - 1)]
        forward.append((count - 1, 0))
        backward = [(target, source) for source, target in forward]
        low = lax.ppermute(
            lax.slice_in_dim(block, block.shape[dim] - width, None, axis=dim), axis, forward
        )
        high = lax.ppermute(lax.slice_in_dim(block, 0, width, axis=dim), axis, backward)
        block = jnp.concatenate([low, block, high], axis=dim)
    return block


def sent_together(arrays, axis, dim, along):
    both = jnp.concatenate(arrays, axis=along)
    filled, at, outs = (lax.all_gather(both, axis, axis=dim, tiled=True), 0, [])
    for a in arrays:
        outs.append(lax.slice_in_dim(filled, at, at + a.shape[along], axis=along))
        at += a.shape[along]
    return tuple(outs)


def split_up(shard, dim, peers):
    lengths = shard.shape
    pieces = shard.reshape(*lengths[:dim], peers, lengths[dim] // peers, *lengths[dim + 1 :])
    return jnp.moveaxis(pieces, dim, 0)


def summed_on_arrival(shard, axis, dim):
    pieces = split_up(shard, dim, lax.axis_size(axis))
    arrived = lax.all_to_all(pieces, axis, split_axis=0, concat_axis=0, tiled=True)
    return arrived.sum(axis=0)


def sum_by_axis(shard, axes, dim):
    far, near = axes
    pieces = split_up(shard, dim, lax.axis_size(far))
    nearer = summed_on_arrival(pieces, near, dim + 1)
    arrived = lax.all_to_all(nearer, far, split_axis=0, concat_axis=0, tiled=True)
    return arrived.sum(axis=0)


def filled_up(lines, peers):
    spare = -lines.shape[0] % peers
    if not spare:
        return lines
    return jnp.concatenate([lines, jnp.zeros((spare, *lines.shape[1:]), lines.dtype)])


def copy_for_each(shard, axis):
    copies = jnp.broadcast_to(shard, (lax.axis_size(axis), *shard.shape))
    return lax.all_to_all(copies, axis, split_axis=0, concat_axis=0, tiled=True)


def in_order(pieces, dim):
    pieces = jnp.moveaxis(pieces, 0, dim)
    lengths = pieces.shape
    return pieces.reshape(*lengths[:dim], lengths[dim] * lengths[dim + 1], *lengths[dim + 2 :])


def gather_axes(shard, axes, dim):
    far, near = axes
    initial = copy_for_each(shard, far)
    pieces = jnp.swapaxes(copy_for_each(initial, near), 0, 1)
    return in_order(pieces.reshape(-1, *shard.shape), dim)


def total_of(shard, axes):
    own = sum_by_axis(filled_up(shard, lax.axis_size(axes[0]) * lax.axis_size(axes[1])), axes, 0)
    whole = gather_axes(own, axes, 0)
    return whole[: len(shard)].reshape(shard.shape)


def packed_total(arrays, axis):
    vector, at, outs = (jnp.concatenate([a.reshape(-1) for a in arrays]), 0, [])
    subtotal = total_of(vector, axis)
    for a in arrays:
        outs.append(subtotal[at : at + a.size].reshape(a.shape))
        at += a.size
    return tuple(outs)


def laplace(field):
    return (
        field[:, 2:, 1:-1]
        + field[:, :-2, 1:-1]
        + field[:, 1:-1, 2:]
        + field[:, 1:-1, :-2]
        - 4.0 * field[:, 1:-1, 1:-1]
    )


def wall_mask(rows_here, width):
    first = lax.axis_index(GY) * rows_here - width
    row_ids = first + jnp.arange(rows_here + 2 * width, dtype=jnp.int32)
    inside = (row_ids >= 0) & (row_ids < rows_here * lax.axis_size(GY))
    return inside.astype(jnp.float32)[None, :, None]


def local(state, u_vel, v_vel, land, forcing, member_mode, theta, obs_index, obs_values, obs_sigma):
    members_here, rows_here, cols_here = state.shape
    ocean = (1 - land).astype(jnp.float32)
    diffuse = (0.05 * (1.0 + 0.5 * jnp.tanh(theta[:, 0])))[:, None, None]
    hyper = (0.005 * (1.0 + 0.5 * jnp.tanh(theta[:, 1])))[:, None, None]
    damping = (0.05 * (1.0 + 0.5 * jnp.tanh(theta[:, 2])))[:, None, None]
    patterns = forcing.shape[0]
    one_hot = (member_mode[:, None] == jnp.arange(patterns, dtype=jnp.int32)[None, :]).astype(
        jnp.float32
    )
    picked = jnp.dot(
        one_hot,
        forcing.reshape(patterns, rows_here * cols_here),
        preferred_element_type=jnp.float32,
        precision=lax.Precision.HIGHEST,
    )
    forced = theta[:, 3][:, None, None] * picked.reshape(members_here, rows_here, cols_here)
    field = state
    wall_one = wall_mask(rows_here, 1)
    wall_two = wall_mask(rows_here, 2)
    for step_index in range(STEPS):
        extended = with_halo(field, (("gx", 2), (GY, 1)), 2) * wall_two
        lap_wide = laplace(extended) * wall_one
        biharm = laplace(lap_wide)
        lap_field = lap_wide[:, 1:-1, 1:-1]
        center = extended[:, 2:-2, 2:-2]
        grad_x = 0.5 * (extended[:, 2:-2, 3:-1] - extended[:, 2:-2, 1:-3])
        grad_y = 0.5 * (extended[:, 3:-1, 2:-2] - extended[:, 1:-3, 2:-2])
        tend = (
            diffuse * lap_field
            - hyper * biharm
            - damping * center
            + forced
            - (u_vel * grad_x + v_vel * grad_y)
        )
        field = (center + tend) * ocean
    site_index = obs_index.reshape(-1)
    observed_here = jnp.take(field.reshape(members_here, rows_here * cols_here), site_index, axis=1)
    observed, theta_all = sent_together((observed_here, theta), "ens", 0, 1)
    sigma = obs_sigma.reshape(-1)
    target = obs_values.reshape(-1)
    anomaly = (observed - jnp.mean(observed, 0)) / sigma
    misfit = (target - observed) / sigma
    total = observed.shape[0]
    start = lax.axis_index("ens") * members_here
    gram_part = jnp.dot(
        anomaly, anomaly.T, preferred_element_type=jnp.float32, precision=lax.Precision.HIGHEST
    )
    cross_part = jnp.dot(
        anomaly, misfit.T, preferred_element_type=jnp.float32, precision=lax.Precision.HIGHEST
    )
    gram, cross_sum = packed_total((gram_part, cross_part), (("gx", "gy_0", "gy_1"), "gy_2"))
    cross_own = lax.dynamic_slice_in_dim(cross_sum, start, members_here, 1)
    system = gram + (total - 1) * jnp.eye(total, dtype=jnp.float32)
    factor = jnp.linalg.cholesky(system)
    weights = jax.scipy.linalg.cho_solve((factor, True), cross_own)
    spread = theta_all - jnp.mean(theta_all, 0)
    new_theta = theta + jnp.dot(
        weights.T, spread, preferred_element_type=jnp.float32, precision=lax.Precision.HIGHEST
    )
    return (field, new_theta)


def solution(mesh):
    torus = Mesh(
        mesh.devices.reshape(mesh.shape["gx"], 2, 4, 2, mesh.shape["ens"]),
        ("gx", "gy_0", "gy_1", "gy_2", "ens"),
    )
    in_specs = (
        P("ens", GY, "gx"),
        P(GY, "gx"),
        P(GY, "gx"),
        P(GY, "gx"),
        P(None, GY, "gx"),
        P("ens"),
        P("ens", None),
        P(GY, "gx", None),
        P(GY, "gx", None),
        P(GY, "gx", None),
    )
    out_specs = (P("ens", GY, "gx"), P("ens", None))
    return jax.shard_map(local, mesh=torus, in_specs=in_specs, out_specs=out_specs, check_vma=False)
```

profile of v0, /device:TPU:1, one launch (start us, length us, event | category | flops | bytes accessed | tf_op | source)
XLA Modules:
  0.0 185.0 jit_solution(16889462870830267027)
XLA Ops:
  0.6 1.2 copy.35
  1.9 0.2 fusion.78
  2.1 2.5 %collective-permute-start = (f32[64,16,2]{2,0,1:T(8,128)S(1)}, f32[64,16,2]{2,0,1:T(8,128)S(1)}, u32[]{:S(2)}, u32[]{:S(2)}) collective-permute-start(f32[64,16,2]{2,0,1:T(8,128)S(1)} %get-tuple-element.24), channel_id=1, source_target_pairs={{0,32},{32,64},{64,96},{96,128},{128,160},{160,192},{192,224},{224... | collective-permute-start | bytes 24584 | tf_op jit(solution)/shard_map/ppermute | solution.py:17
  4.6 4.0 %collective-permute-start.1 = (f32[64,16,2]{2,0,1:T(8,128)S(1)}, f32[64,16,2]{2,0,1:T(8,128)S(1)}, u32[]{:S(2)}, u32[]{:S(2)}) collective-permute-start(f32[64,16,2]{2,0,1:T(8,128)S(1)} %get-tuple-element.25), channel_id=1, source_target_pairs={{32,0},{64,32},{96,64},{128,96},{160,128},{192,160},{224,192},{0,2... | collective-permute-start | bytes 24584 | tf_op jit(solution)/shard_map/ppermute | solution.py:20
  8.8 11.4 %collective-permute-done = f32[64,16,2]{2,0,1:T(8,128)S(1)} collective-permute-done((f32[64,16,2]{2,0,1:T(8,128)S(1)}, f32[64,16,2]{2,0,1:T(8,128)S(1)}, u32[]{:S(2)}, u32[]{:S(2)}) %collective-permute-start) | collective-permute-done | bytes 8224 | tf_op jit(solution)/shard_map/ppermute | solution.py:17
  20.4 2.4 %collective-permute-start.2 = (f32[64,2,132]{2,0,1:T(8,128)S(1)}, f32[64,2,132]{2,0,1:T(8,128)S(1)}, u32[]{:S(2)}, u32[]{:S(2)}) collective-permute-start(f32[64,2,132]{2,0,1:T(8,128)S(1)} %get-tuple-element.16), channel_id=1, source_target_pairs={{0,2},{2,4},{4,6},{6,8},{8,10},{10,12},{12,14},{14,16},{16,18},{18... | collective-permute-start | bytes 202760 | tf_op jit(solution)/shard_map/ppermute | solution.py:17
  22.8 1.9 %collective-permute-done.2 = f32[64,2,132]{2,0,1:T(8,128)S(1)} collective-permute-done((f32[64,2,132]{2,0,1:T(8,128)S(1)}, f32[64,2,132]{2,0,1:T(8,128)S(1)}, u32[]{:S(2)}, u32[]{:S(2)}) %collective-permute-start.2) | collective-permute-done | bytes 67616 | tf_op jit(solution)/shard_map/ppermute | solution.py:17
  24.7 2.7 %collective-permute-done.3 = f32[64,2,132]{2,0,1:T(8,128)S(1)} collective-permute-done((f32[64,2,132]{2,0,1:T(8,128)S(1)}, f32[64,2,132]{2,0,1:T(8,128)S(1)}, u32[]{:S(2)}, u32[]{:S(2)}) %collective-permute-start.3) | collective-permute-done | bytes 67616 | tf_op jit(solution)/shard_map/ppermute | solution.py:20
  27.5 0.5 maximum_multiply_fusion
  28.0 1.3 fusion.7
  29.3 1.5 fusion.45
  31.1 2.8 %collective-permute-start.5 = (f32[64,16,2]{2,0,1:T(8,128)S(1)}, f32[64,16,2]{2,0,1:T(8,128)S(1)}, u32[]{:S(2)}, u32[]{:S(2)}) collective-permute-start(f32[64,16,2]{2,0,1:T(8,128)S(1)} %get-tuple-element.23), channel_id=1, source_target_pairs={{32,0},{64,32},{96,64},{128,96},{160,128},{192,160},{224,192},{0,2... | collective-permute-start | bytes 24584 | tf_op jit(solution)/shard_map/ppermute | solution.py:20
  33.9 9.8 %collective-permute-done.4 = f32[64,16,2]{2,0,1:T(8,128)S(1)} collective-permute-done((f32[64,16,2]{2,0,1:T(8,128)S(1)}, f32[64,16,2]{2,0,1:T(8,128)S(1)}, u32[]{:S(2)}, u32[]{:S(2)}) %collective-permute-start.4) | collective-permute-done | bytes 8224 | tf_op jit(solution)/shard_map/ppermute | solution.py:17
  43.9 2.4 %collective-permute-start.6 = (f32[64,2,132]{2,0,1:T(8,128)S(1)}, f32[64,2,132]{2,0,1:T(8,128)S(1)}, u32[]{:S(2)}, u32[]{:S(2)}) collective-permute-start(f32[64,2,132]{2,0,1:T(8,128)S(1)} %get-tuple-element.14), channel_id=1, source_target_pairs={{0,2},{2,4},{4,6},{6,8},{8,10},{10,12},{12,14},{14,16},{16,18},{18... | collective-permute-start | bytes 202760 | tf_op jit(solution)/shard_map/ppermute | solution.py:17
  46.3 0.9 collective-permute-start.7
  47.2 1.0 collective-permute-done.6
  48.3 2.4 %collective-permute-done.7 = f32[64,2,132]{2,0,1:T(8,128)S(1)} collective-permute-done((f32[64,2,132]{2,0,1:T(8,128)S(1)}, f32[64,2,132]{2,0,1:T(8,128)S(1)}, u32[]{:S(2)}, u32[]{:S(2)}) %collective-permute-start.7) | collective-permute-done | bytes 67616 | tf_op jit(solution)/shard_map/ppermute | solution.py:20
  50.7 0.5 maximum_multiply_fusion.1
  51.2 1.3 fusion.5
  52.5 1.3 fusion.34
  53.9 0.2 fusion.76
  54.1 2.3 %collective-permute-start.8 = (f32[64,16,2]{2,0,1:T(8,128)S(1)}, f32[64,16,2]{2,0,1:T(8,128)S(1)}, u32[]{:S(2)}, u32[]{:S(2)}) collective-permute-start(f32[64,16,2]{2,0,1:T(8,128)S(1)} %get-tuple-element.20), channel_id=1, source_target_pairs={{0,32},{32,64},{64,96},{96,128},{128,160},{160,192},{192,224},{224... | collective-permute-start | bytes 24584 | tf_op jit(solution)/shard_map/ppermute | solution.py:17
  56.4 1.0 collective-permute-start.9
  57.4 8.2 %collective-permute-done.8 = f32[64,16,2]{2,0,1:T(8,128)S(1)} collective-permute-done((f32[64,16,2]{2,0,1:T(8,128)S(1)}, f32[64,16,2]{2,0,1:T(8,128)S(1)}, u32[]{:S(2)}, u32[]{:S(2)}) %collective-permute-start.8) | collective-permute-done | bytes 8224 | tf_op jit(solution)/shard_map/ppermute | solution.py:17
  65.5 1.1 collective-permute-done.9
  66.8 4.3 %collective-permute-start.10 = (f32[64,2,132]{2,0,1:T(8,128)S(1)}, f32[64,2,132]{2,0,1:T(8,128)S(1)}, u32[]{:S(2)}, u32[]{:S(2)}) collective-permute-start(f32[64,2,132]{2,0,1:T(8,128)S(1)} %get-tuple-element.12), channel_id=1, source_target_pairs={{0,2},{2,4},{4,6},{6,8},{8,10},{10,12},{12,14},{14,16},{16,18},{18... | collective-permute-start | bytes 202760 | tf_op jit(solution)/shard_map/ppermute | solution.py:17
  71.1 0.6 collective-permute-start.11
  71.6 1.4 collective-permute-done.10
  73.0 2.4 %collective-permute-done.11 = f32[64,2,132]{2,0,1:T(8,128)S(1)} collective-permute-done((f32[64,2,132]{2,0,1:T(8,128)S(1)}, f32[64,2,132]{2,0,1:T(8,128)S(1)}, u32[]{:S(2)}, u32[]{:S(2)}) %collective-permute-start.11) | collective-permute-done | bytes 67616 | tf_op jit(solution)/shard_map/ppermute | solution.py:20
  75.5 0.5 maximum_multiply_fusion.2
  76.0 1.3 fusion.3
  77.3 1.3 fusion.23
  78.6 0.2 fusion.75
  78.8 2.1 %collective-permute-start.12 = (f32[64,16,2]{2,0,1:T(8,128)S(1)}, f32[64,16,2]{2,0,1:T(8,128)S(1)}, u32[]{:S(2)}, u32[]{:S(2)}) collective-permute-start(f32[64,16,2]{2,0,1:T(8,128)S(1)} %get-tuple-element.18), channel_id=1, source_target_pairs={{0,32},{32,64},{64,96},{96,128},{128,160},{160,192},{192,224},{224... | collective-permute-start | bytes 24584 | tf_op jit(solution)/shard_map/ppermute | solution.py:17
  80.9 0.7 collective-permute-start.13
  81.6 7.9 %collective-permute-done.12 = f32[64,16,2]{2,0,1:T(8,128)S(1)} collective-permute-done((f32[64,16,2]{2,0,1:T(8,128)S(1)}, f32[64,16,2]{2,0,1:T(8,128)S(1)}, u32[]{:S(2)}, u32[]{:S(2)}) %collective-permute-start.12) | collective-permute-done | bytes 8224 | tf_op jit(solution)/shard_map/ppermute | solution.py:17
  89.5 1.1 collective-permute-done.13
  90.8 5.0 %collective-permute-start.14 = (f32[64,2,132]{2,0,1:T(8,128)S(1)}, f32[64,2,132]{2,0,1:T(8,128)S(1)}, u32[]{:S(2)}, u32[]{:S(2)}) collective-permute-start(f32[64,2,132]{2,0,1:T(8,128)S(1)} %get-tuple-element.10), channel_id=1, source_target_pairs={{0,2},{2,4},{4,6},{6,8},{8,10},{10,12},{12,14},{14,16},{16,18},{18... | collective-permute-start | bytes 202760 | tf_op jit(solution)/shard_map/ppermute | solution.py:17
  95.8 1.9 %collective-permute-done.14 = f32[64,2,132]{2,0,1:T(8,128)S(1)} collective-permute-done((f32[64,2,132]{2,0,1:T(8,128)S(1)}, f32[64,2,132]{2,0,1:T(8,128)S(1)}, u32[]{:S(2)}, u32[]{:S(2)}) %collective-permute-start.14) | collective-permute-done | bytes 67616 | tf_op jit(solution)/shard_map/ppermute | solution.py:17
  97.8 2.4 %collective-permute-done.15 = f32[64,2,132]{2,0,1:T(8,128)S(1)} collective-permute-done((f32[64,2,132]{2,0,1:T(8,128)S(1)}, f32[64,2,132]{2,0,1:T(8,128)S(1)}, u32[]{:S(2)}, u32[]{:S(2)}) %collective-permute-start.15) | collective-permute-done | bytes 67616 | tf_op jit(solution)/shard_map/ppermute | solution.py:20
  100.2 0.5 maximum_multiply_fusion.3
  100.7 1.3 fusion.1
  102.0 1.3 fusion.12
  103.4 0.3 copy.47
  103.7 0.6 gather_fusion
  104.5 3.8 %all_gather.3 = f32[128,132]{1,0:T(8,128)S(1)} all-gather(f32[64,132]{1,0:T(8,128)S(1)} %copy.40), channel_id=1, replica_groups=mesh['gx'=8,'gy_0'=2,'gy_1'=4,'gy_2'=2,'ens'=2] {'ens'}, dimensions={0}, use_global_device_ids=true | all-gather | bytes 101376 | tf_op jit(solution)/shard_map/all_gather | solution.py:27
  108.4 0.3 fusion.69
  108.7 0.3 fusion.61
  109.1 8.0 %all_to_all.28 = f32[2,64,256]{2,1,0:T(8,128)S(1)} all-to-all(f32[2,64,256]{2,1,0:T(8,128)S(1)} %maximum_bitcast_fusion), channel_id=1, replica_groups=mesh['gx'=8,'gy_0'=2,'gy_1'=4,'gy_2'=2,'ens'=2] {'gy_2'}, dimensions={0} | all-to-all | bytes 262144 | tf_op jit(solution)/shard_map/all_to_all | solution.py:42
  117.0 0.7 all_to_all.19
  117.7 8.9 %all-to-all-start.1 = ((f32[64,1,256]{2,1,0:T(1,128)}), f32[64,1,256]{2,1,0:T(1,128)S(1)}, u32[]{:S(2)}, u32[]{:S(2)}) async-start(f32[64,1,256]{2,1,0:T(1,128)} %all_to_all.19), calls=%async_computation.1 | async-start | bytes 131072 | tf_op jit(solution)/shard_map/all_to_all | solution.py:50
  126.6 1.1 copy.46
  127.7 9.8 %all-to-all-done.1 = f32[64,1,256]{2,1,0:T(1,128)S(1)} async-done(((f32[64,1,256]{2,1,0:T(1,128)}), f32[64,1,256]{2,1,0:T(1,128)S(1)}, u32[]{:S(2)}, u32[]{:S(2)}) %all-to-all-start.1) | async-done | bytes 65568 | tf_op jit(solution)/shard_map/all_to_all | solution.py:50
  137.6 0.7 broadcast_in_dim.14
  138.2 4.6 %all-to-all-start.2 = ((f32[64,1,256]{2,1,0:T(1,128)}), f32[64,1,256]{2,1,0:T(1,128)S(1)}, u32[]{:S(2)}, u32[]{:S(2)}) async-start(f32[64,1,256]{2,1,0:T(1,128)} %broadcast_in_dim.14), calls=%async_computation.2 | async-start | bytes 131072 | tf_op jit(solution)/shard_map/all_to_all | solution.py:63
  142.9 11.0 %all-to-all-done.2 = f32[64,1,256]{2,1,0:T(1,128)S(1)} async-done(((f32[64,1,256]{2,1,0:T(1,128)}), f32[64,1,256]{2,1,0:T(1,128)S(1)}, u32[]{:S(2)}, u32[]{:S(2)}) %all-to-all-start.2) | async-done | bytes 65568 | tf_op jit(solution)/shard_map/all_to_all | solution.py:63
  153.8 6.5 %all_to_all.29 = f32[2,64,256]{2,1,0:T(8,128)S(1)} all-to-all(f32[2,64,256]{2,1,0:T(8,128)S(1)} %broadcast_in_dim.15), channel_id=1, replica_groups=mesh['gx'=8,'gy_0'=2,'gy_1'=4,'gy_2'=2,'ens'=2] {'gy_2'}, dimensions={0} | all-to-all | bytes 262144 | tf_op jit(solution)/shard_map/all_to_all | solution.py:63
  160.6 11.7 %cholesky.16 = f32[128,128]{1,0:T(8,128)S(1)} custom-call(f32[128,128]{1,0:T(8,128)S(1)} %fusion.58), custom_call_target="Cholesky" | custom-call | tf_op jit(solution)/shard_map/jit(cholesky)/cholesky | solution.py:165
  172.4 0.6 compare_reduce_fusion
  173.0 0.7 fusion.52
  173.7 9.8 %custom-call.10 = f32[1,128,128]{1,2,0:T(8,128)S(1)} custom-call(f32[1,128,128]{2,1,0:T(8,128)S(1)} %fusion.52), custom_call_target="InvertDiagBlocksLowerTriangular" | custom-call | tf_op jit(solution)/shard_map/jit(_cho_solve)/triangular_solve | solution.py:166
  183.6 0.3 fusion.56
  184.0 0.2 fusion.54
  184.2 0.8 convolution_add_fusion
  (61 shorter events, 1.9 us)
Async XLA Ops:
  1.8 6.8 %copy-start = (f32[64,4]{0,1:T(4,128)S(1)}, f32[64,4]{0,1:T(4,128)}, u32[]{:S(2)}) copy-start(f32[64,4]{0,1:T(4,128)} %param.16) | copy-start | bytes 3076
  1.9 6.8 %copy-start.1 = (s32[16,128]{1,0:T(8,128)S(1)}, s32[16,128]{1,0:T(8,128)}, u32[]{:S(2)}) copy-start(s32[16,128]{1,0:T(8,128)} %param.13) | copy-start | bytes 24580
  1.9 6.8 %copy-start.2 = (f32[16,128]{1,0:T(8,128)S(1)}, f32[16,128]{1,0:T(8,128)}, u32[]{:S(2)}) copy-start(f32[16,128]{1,0:T(8,128)} %param.12) | copy-start | bytes 24580
  1.9 6.8 %copy-start.3 = (f32[16,128]{1,0:T(8,128)S(1)}, f32[16,128]{1,0:T(8,128)}, u32[]{:S(2)}) copy-start(f32[16,128]{1,0:T(8,128)} %param.11) | copy-start | bytes 24580
  2.1 18.1 %collective-permute-start = (f32[64,16,2]{2,0,1:T(8,128)S(1)}, f32[64,16,2]{2,0,1:T(8,128)S(1)}, u32[]{:S(2)}, u32[]{:S(2)}) collective-permute-start(f32[64,16,2]{2,0,1:T(8,128)S(1)} %get-tuple-element.24), channel_id=1, source_target_pairs={{0,32},{32,64},{64,96},{96,128},{128,160},{160,192},{192,224},{224... | collective-permute-start | bytes 24584 | tf_op jit(solution)/shard_map/ppermute | solution.py:17
  4.6 15.6 %collective-permute-start.1 = (f32[64,16,2]{2,0,1:T(8,128)S(1)}, f32[64,16,2]{2,0,1:T(8,128)S(1)}, u32[]{:S(2)}, u32[]{:S(2)}) collective-permute-start(f32[64,16,2]{2,0,1:T(8,128)S(1)} %get-tuple-element.25), channel_id=1, source_target_pairs={{32,0},{64,32},{96,64},{128,96},{160,128},{192,160},{224,192},{0,2... | collective-permute-start | bytes 24584 | tf_op jit(solution)/shard_map/ppermute | solution.py:20
  20.4 4.4 %collective-permute-start.2 = (f32[64,2,132]{2,0,1:T(8,128)S(1)}, f32[64,2,132]{2,0,1:T(8,128)S(1)}, u32[]{:S(2)}, u32[]{:S(2)}) collective-permute-start(f32[64,2,132]{2,0,1:T(8,128)S(1)} %get-tuple-element.16), channel_id=1, source_target_pairs={{0,2},{2,4},{4,6},{6,8},{8,10},{10,12},{12,14},{14,16},{16,18},{18... | collective-permute-start | bytes 202760 | tf_op jit(solution)/shard_map/ppermute | solution.py:17
  22.8 4.7 %collective-permute-start.3 = (f32[64,2,132]{2,0,1:T(8,128)S(1)}, f32[64,2,132]{2,0,1:T(8,128)S(1)}, u32[]{:S(2)}, u32[]{:S(2)}) collective-permute-start(f32[64,2,132]{2,0,1:T(8,128)S(1)} %get-tuple-element.17), channel_id=1, source_target_pairs={{2,0},{4,2},{6,4},{8,6},{10,8},{12,10},{14,12},{16,14},{18,16},{20... | collective-permute-start | bytes 202760 | tf_op jit(solution)/shard_map/ppermute | solution.py:20
  28.0 1.3 copy-start.4
  28.0 1.3 copy-start.5
  31.0 12.7 %collective-permute-start.4 = (f32[64,16,2]{2,0,1:T(8,128)S(1)}, f32[64,16,2]{2,0,1:T(8,128)S(1)}, u32[]{:S(2)}, u32[]{:S(2)}) collective-permute-start(f32[64,16,2]{2,0,1:T(8,128)S(1)} %get-tuple-element.22), channel_id=1, source_target_pairs={{0,32},{32,64},{64,96},{96,128},{128,160},{160,192},{192,224},{224... | collective-permute-start | bytes 24584 | tf_op jit(solution)/shard_map/ppermute | solution.py:17
  31.1 12.6 %collective-permute-start.5 = (f32[64,16,2]{2,0,1:T(8,128)S(1)}, f32[64,16,2]{2,0,1:T(8,128)S(1)}, u32[]{:S(2)}, u32[]{:S(2)}) collective-permute-start(f32[64,16,2]{2,0,1:T(8,128)S(1)} %get-tuple-element.23), channel_id=1, source_target_pairs={{32,0},{64,32},{96,64},{128,96},{160,128},{192,160},{224,192},{0,2... | collective-permute-start | bytes 24584 | tf_op jit(solution)/shard_map/ppermute | solution.py:20
  43.9 4.4 %collective-permute-start.6 = (f32[64,2,132]{2,0,1:T(8,128)S(1)}, f32[64,2,132]{2,0,1:T(8,128)S(1)}, u32[]{:S(2)}, u32[]{:S(2)}) collective-permute-start(f32[64,2,132]{2,0,1:T(8,128)S(1)} %get-tuple-element.14), channel_id=1, source_target_pairs={{0,2},{2,4},{4,6},{6,8},{8,10},{10,12},{12,14},{14,16},{16,18},{18... | collective-permute-start | bytes 202760 | tf_op jit(solution)/shard_map/ppermute | solution.py:17
  46.3 4.4 %collective-permute-start.7 = (f32[64,2,132]{2,0,1:T(8,128)S(1)}, f32[64,2,132]{2,0,1:T(8,128)S(1)}, u32[]{:S(2)}, u32[]{:S(2)}) collective-permute-start(f32[64,2,132]{2,0,1:T(8,128)S(1)} %get-tuple-element.15), channel_id=1, source_target_pairs={{2,0},{4,2},{6,4},{8,6},{10,8},{12,10},{14,12},{16,14},{18,16},{20... | collective-permute-start | bytes 202760 | tf_op jit(solution)/shard_map/ppermute | solution.py:20
  54.1 17.6 %copy-start.6 = (s32[1,1,128]{2,1,0:T(1,128)S(1)}, s32[1,1,128]{2,1,0:T(1,128)}, u32[]{:S(2)}) copy-start(s32[1,1,128]{2,1,0:T(1,128)} %param.17) | copy-start | bytes 1540
  54.1 11.5 %collective-permute-start.8 = (f32[64,16,2]{2,0,1:T(8,128)S(1)}, f32[64,16,2]{2,0,1:T(8,128)S(1)}, u32[]{:S(2)}, u32[]{:S(2)}) collective-permute-start(f32[64,16,2]{2,0,1:T(8,128)S(1)} %get-tuple-element.20), channel_id=1, source_target_pairs={{0,32},{32,64},{64,96},{96,128},{128,160},{160,192},{192,224},{224... | collective-permute-start | bytes 24584 | tf_op jit(solution)/shard_map/ppermute | solution.py:17
  56.4 10.2 %collective-permute-start.9 = (f32[64,16,2]{2,0,1:T(8,128)S(1)}, f32[64,16,2]{2,0,1:T(8,128)S(1)}, u32[]{:S(2)}, u32[]{:S(2)}) collective-permute-start(f32[64,16,2]{2,0,1:T(8,128)S(1)} %get-tuple-element.21), channel_id=1, source_target_pairs={{32,0},{64,32},{96,64},{128,96},{160,128},{192,160},{224,192},{0,2... | collective-permute-start | bytes 24584 | tf_op jit(solution)/shard_map/ppermute | solution.py:20
  66.8 6.2 %collective-permute-start.10 = (f32[64,2,132]{2,0,1:T(8,128)S(1)}, f32[64,2,132]{2,0,1:T(8,128)S(1)}, u32[]{:S(2)}, u32[]{:S(2)}) collective-permute-start(f32[64,2,132]{2,0,1:T(8,128)S(1)} %get-tuple-element.12), channel_id=1, source_target_pairs={{0,2},{2,4},{4,6},{6,8},{8,10},{10,12},{12,14},{14,16},{16,18},{18... | collective-permute-start | bytes 202760 | tf_op jit(solution)/shard_map/ppermute | solution.py:17
  71.1 4.4 %collective-permute-start.11 = (f32[64,2,132]{2,0,1:T(8,128)S(1)}, f32[64,2,132]{2,0,1:T(8,128)S(1)}, u32[]{:S(2)}, u32[]{:S(2)}) collective-permute-start(f32[64,2,132]{2,0,1:T(8,128)S(1)} %get-tuple-element.13), channel_id=1, source_target_pairs={{2,0},{4,2},{6,4},{8,6},{10,8},{12,10},{14,12},{16,14},{18,16},{20... | collective-permute-start | bytes 202760 | tf_op jit(solution)/shard_map/ppermute | solution.py:20
  78.8 10.7 %collective-permute-start.12 = (f32[64,16,2]{2,0,1:T(8,128)S(1)}, f32[64,16,2]{2,0,1:T(8,128)S(1)}, u32[]{:S(2)}, u32[]{:S(2)}) collective-permute-start(f32[64,16,2]{2,0,1:T(8,128)S(1)} %get-tuple-element.18), channel_id=1, source_target_pairs={{0,32},{32,64},{64,96},{96,128},{128,160},{160,192},{192,224},{224... | collective-permute-start | bytes 24584 | tf_op jit(solution)/shard_map/ppermute | solution.py:17
  80.9 9.7 %collective-permute-start.13 = (f32[64,16,2]{2,0,1:T(8,128)S(1)}, f32[64,16,2]{2,0,1:T(8,128)S(1)}, u32[]{:S(2)}, u32[]{:S(2)}) collective-permute-start(f32[64,16,2]{2,0,1:T(8,128)S(1)} %get-tuple-element.19), channel_id=1, source_target_pairs={{32,0},{64,32},{96,64},{128,96},{160,128},{192,160},{224,192},{0,2... | collective-permute-start | bytes 24584 | tf_op jit(solution)/shard_map/ppermute | solution.py:20
  90.8 7.0 %collective-permute-start.14 = (f32[64,2,132]{2,0,1:T(8,128)S(1)}, f32[64,2,132]{2,0,1:T(8,128)S(1)}, u32[]{:S(2)}, u32[]{:S(2)}) collective-permute-start(f32[64,2,132]{2,0,1:T(8,128)S(1)} %get-tuple-element.10), channel_id=1, source_target_pairs={{0,2},{2,4},{4,6},{6,8},{8,10},{10,12},{12,14},{14,16},{16,18},{18... | collective-permute-start | bytes 202760 | tf_op jit(solution)/shard_map/ppermute | solution.py:17
  95.8 4.4 %collective-permute-start.15 = (f32[64,2,132]{2,0,1:T(8,128)S(1)}, f32[64,2,132]{2,0,1:T(8,128)S(1)}, u32[]{:S(2)}, u32[]{:S(2)}) collective-permute-start(f32[64,2,132]{2,0,1:T(8,128)S(1)} %get-tuple-element.11), channel_id=1, source_target_pairs={{2,0},{4,2},{6,4},{8,6},{10,8},{12,10},{14,12},{16,14},{18,16},{20... | collective-permute-start | bytes 202760 | tf_op jit(solution)/shard_map/ppermute | solution.py:20
  103.3 5.0 %copy-start.8 = (f32[1,1,128]{2,1,0:T(1,128)S(1)}, f32[1,1,128]{2,1,0:T(1,128)}, u32[]{:S(2)}) copy-start(f32[1,1,128]{2,1,0:T(1,128)} %param.19) | copy-start | bytes 1540
  103.4 5.4 %copy-start.7 = (f32[1,1,128]{2,1,0:T(1,128)S(1)}, f32[1,1,128]{2,1,0:T(1,128)}, u32[]{:S(2)}) copy-start(f32[1,1,128]{2,1,0:T(1,128)} %param.18) | copy-start | bytes 1540
  117.7 19.8 %all-to-all-start.1 = ((f32[64,1,256]{2,1,0:T(1,128)}), f32[64,1,256]{2,1,0:T(1,128)S(1)}, u32[]{:S(2)}, u32[]{:S(2)}) async-start(f32[64,1,256]{2,1,0:T(1,128)} %all_to_all.19), calls=%async_computation.1 | async-start | bytes 131072 | tf_op jit(solution)/shard_map/all_to_all | solution.py:50
  138.2 15.6 %all-to-all-start.2 = ((f32[64,1,256]{2,1,0:T(1,128)}), f32[64,1,256]{2,1,0:T(1,128)S(1)}, u32[]{:S(2)}, u32[]{:S(2)}) async-start(f32[64,1,256]{2,1,0:T(1,128)} %broadcast_in_dim.14), calls=%async_computation.2 | async-start | bytes 131072 | tf_op jit(solution)/shard_map/all_to_all | solution.py:63
where the time goes:
time: 185 us
  waiting for transfers between devices  76.6 us (41%)
  starting transfers between devices  44.7 us (24%)
  other arithmetic  35 us (19%)
  blocking collectives  18.2 us (10%)
  local copies, waits for them, and re-layouts  6 us (3%)
  matrix products  3.42 us (2%)
    ppermute x8, waiting for transfers between devices, with_halo(): lax.ppermute(lax.slice_in_dim(block, block.shape[dim] - width, None, axis...  43.6 us
    ppermute x8, starting transfers between devices, with_halo(): lax.ppermute(lax.slice_in_dim(block, block.shape[dim] - width, None, axis...  21.2 us
    another operation x3, other arithmetic, local(): factor = jnp.linalg.cholesky(system)  12.4 us
    ppermute x8, waiting for transfers between devices, with_halo(): lax.ppermute(lax.slice_in_dim(block, 0, width, axis=dim), axis, backward)  12.3 us
    all_to_all x1, waiting for transfers between devices, copy_for_each(): return lax.all_to_all(copies, axis, split_axis=0, concat_axis=0, tiled=True)  11 us
    another operation x2, other arithmetic, local(): weights = jax.scipy.linalg.cho_solve((factor, True), cross_own)  10.5 us
    ppermute x8, starting transfers between devices, with_halo(): lax.ppermute(lax.slice_in_dim(block, 0, width, axis=dim), axis, backward)  9.98 us
    all_to_all x1, waiting for transfers between devices, sum_by_axis(): lax.all_to_all(nearer, far, split_axis=0, concat_axis=0, tiled=True)  9.78 us
  transfers between devices with their start and end apart: 18, of which 16 were waited for; matrix products, arithmetic and copies ran while one was open for 1% of the time, Pallas kernels for 0%

commit v1 on v0

v1 whole, which is shorter than its diff:
```python
import jax
import jax.numpy as jnp
from jax import lax
from jax.experimental import pallas as pl
from jax.experimental.pallas import tpu as pltpu
from jax.sharding import PartitionSpec as P

STEPS = 4
W = 2 * STEPS
MESH = pl.DeviceIdType.MESH
F32 = jnp.float32
HIGHEST = lax.Precision.HIGHEST
CHUNK = 16


def iota(shape, dim):
    return lax.broadcasted_iota(jnp.int32, shape, dim)


def pack_edges(ref, first, rows, count, r_ref, l_ref, group):
    lo, hi = rows
    slot = iota((hi - lo, 128), 1) // 16
    for n in range(count):
        right = left = None
        for k in range(8):
            x = ref[first + 8 * n + k, lo:hi, :]
            a = pltpu.roll(x, (16 * (k + 1)) % 128, 1) if k < 7 else x
            b = pltpu.roll(x, 16 * k, 1) if k else x
            right = a if right is None else jnp.where(slot == k, a, right)
            left = b if left is None else jnp.where(slot == k, b, left)
        r_ref[group + n, lo:hi, :] = right
        l_ref[group + n, lo:hi, :] = left


def strips_of(rv, lv, rvr, lvr, lo, hi):
    inner = iota((hi - lo, 128), 1) % 32 < 16
    left = (
        jnp.where(inner, rvr, pltpu.roll(lv, 16, 1)),
        jnp.where(inner, pltpu.roll(rvr, 112, 1), lv),
    )
    right = (
        jnp.where(inner, rv, pltpu.roll(lvr, 16, 1)),
        jnp.where(inner, pltpu.roll(rv, 112, 1), lvr),
    )
    return left, right


def advance(first, planes, coef, tables, forced, qs, lqs, es, mask, put):
    c0, c1, hy = coef
    ocean, uo, vo = tables
    for step in range(STEPS):
        lo = 2 * step
        nl = 4 * W - 2 - 4 * step
        nn = nl - 2
        for p in range(planes):
            get = (lambda a, n, p=p: first(p, a, n)) if step == 0 else (lambda a, n, p=p: qs[p, a : a + n, :])
            cen = get(lo + 1, nl)
            west = pltpu.roll(cen, 1, 1)
            east = pltpu.roll(cen, 127, 1)
            lap = (get(lo + 2, nl) + get(lo, nl)) + (west + east) - 4.0 * cen
            lqs[p, lo + 1 : lo + 1 + nl, :] = lap * mask[lo + 1 : lo + 1 + nl, :]
            es[p, lo + 1 : lo + 1 + nl, :] = east - west
        at = slice(lo + 2, lo + 2 + nn)
        for p in range(planes):
            get = (lambda a, n, p=p: first(p, a, n)) if step == 0 else (lambda a, n, p=p: qs[p, a : a + n, :])
            lap = lqs[p, at, :]
            around = (lqs[p, lo + 3 : lo + 3 + nn, :] + lqs[p, lo + 1 : lo + 1 + nn, :]) + (
                pltpu.roll(lap, 1, 1) + pltpu.roll(lap, 127, 1)
            )
            dy = get(lo + 3, nn) - get(lo + 1, nn)
            inner = c0(p) * get(lo + 2, nn) + c1(p) * lap - hy(p) * around + forced(p, lo + 2, nn)
            new = ocean(p, lo + 2, nn) * inner - (
                uo(p, lo + 2, nn) * es[p, at, :] + vo(p, lo + 2, nn) * dy
            )
            if step < STEPS - 1:
                qs[p, at, :] = new
            else:
                put(p, new)


def kernel(
    mode, state, u_vel, v_vel, land, forcing, theta, obs_index, obs_values, obs_sigma,
    fin_out, theta_out,
    qx, ex, landb, rv, lv, rvr, lvr, mask, tabs, ftab, stabs, coefs, pcoefs,
    qs, lqs, es, fos, qp, qps, lqps, eps, fops, endp, fin, oall, thx, thr,
    gp, rs, zs, ag, mat,
    lsem, osem, hs, hr, xs, xr, rss, rsr, zss, zsr, ags, agr,
):
    z, g, e = lax.axis_index("gx"), lax.axis_index("gy"), lax.axis_index("ens")
    nz, ng = 8, 16
    up_ok, down_ok = g > 0, g < ng - 1

    def dev(dz, dg):
        return {"gx": lax.rem(z + dz + nz, nz), "gy": lax.rem(g + dg + ng, ng), "ens": e}

    pair = {"gx": z, "gy": g, "ens": 1 - e}
    barrier = pltpu.get_barrier_semaphore()
    partners = [dev(0, d) for d in range(1, ng)] + [dev(d, 0) for d in range(1, nz)] + [pair]
    partners += [dev(a, b) for a in (-1, 1) for b in (-1, 1)]
    for where in partners:
        pl.semaphore_signal(barrier, inc=1, device_id=where, device_id_type=MESH)

    own = pl.ds(W, 16)
    loads = [
        pltpu.make_async_copy(state, qx.at[:, own, :], lsem.at[0]),
        pltpu.make_async_copy(forcing, ex.at[0:8, own, :], lsem.at[1]),
        pltpu.make_async_copy(u_vel, ex.at[8, own, :], lsem.at[2]),
        pltpu.make_async_copy(v_vel, ex.at[9, own, :], lsem.at[3]),
        pltpu.make_async_copy(land, landb, lsem.at[4]),
    ]
    for c in loads:
        c.start()

    lane64 = iota((64, 128), 1)
    diag = lane64 == iota((64, 128), 0) + 64 * e
    tt = theta[...]
    th = jnp.tanh(tt)
    spread4 = [jnp.broadcast_to(th[:, p : p + 1], (64, 128)) for p in range(3)]
    raw4 = [jnp.broadcast_to(tt[:, p : p + 1], (64, 128)) for p in range(4)]
    hyper = 0.005 * (1.0 + 0.5 * spread4[1])
    coefs[0] = 1.0 - 0.05 * (1.0 + 0.5 * spread4[2])
    coefs[1] = 0.05 * (1.0 + 0.5 * spread4[0]) + 4.0 * hyper
    coefs[2] = hyper
    coefs[3] = raw4[3]
    thx[...] = jnp.zeros((8, 128), F32)
    for p in range(4):
        thx[p : p + 1, :] = jnp.sum(jnp.where(diag, raw4[p], 0.0), axis=0, keepdims=True)
    slot8 = iota((8, 128), 1) // 32
    for t in range(4):
        for odd in range(2):
            acc = None
            for k in range(4):
                x = coefs[t, pl.ds(odd + 2 * k, 8, stride=8), :]
                acc = x if acc is None else jnp.where(slot8 == k, x, acc)
            pcoefs[t, odd] = acc
    row32 = iota((32, 128), 0)
    no_wall = (jnp.logical_or(row32 >= W, up_ok)) & (jnp.logical_or(row32 < W + 16, down_ok))
    mask[...] = no_wall.astype(F32)

    for c in loads[1:]:
        c.wait()
    ex[10, W : W + 16, :] = (1 - landb[...]).astype(F32)
    ex[11:16, W : W + 16, :] = jnp.zeros((5, 16, 128), F32)

    @pl.when(jnp.logical_not(up_ok))
    def _():
        for ref in (qx, ex, rvr, lvr):
            ref[:, 0:W, :] = jnp.zeros((ref.shape[0], W, 128), F32)

    @pl.when(jnp.logical_not(down_ok))
    def _():
        for ref in (qx, ex, rvr, lvr):
            ref[:, W + 16 :, :] = jnp.zeros((ref.shape[0], W, 128), F32)

    pack_edges(ex, 0, (W, W + 16), 2, rv, lv, 8)
    loads[0].wait()

    def pack_own(c, carry):
        pack_edges(qx, 16 * c, (W, W + 16), 2, rv, lv, 2 * c)
        return carry

    lax.fori_loop(0, 4, pack_own, 0)

    top, bottom, low, high = pl.ds(W, W), pl.ds(16, W), pl.ds(0, W), pl.ds(W + 16, W)

    def halo(c, planes, first, group):
        at, ga = pl.ds(first, 16), pl.ds(group, 2)
        plan = [
            (planes, at, top, planes, high, (0, -1), up_ok, down_ok),
            (planes, at, bottom, planes, low, (0, 1), down_ok, up_ok),
            (rv, ga, own, rvr, own, (1, 0), None, None),
            (lv, ga, own, lvr, own, (-1, 0), None, None),
            (rv, ga, bottom, rvr, low, (1, 1), down_ok, up_ok),
            (rv, ga, top, rvr, high, (1, -1), up_ok, down_ok),
            (lv, ga, bottom, lvr, low, (-1, 1), down_ok, up_ok),
            (lv, ga, top, lvr, high, (-1, -1), up_ok, down_ok),
        ]
        out = []
        for i, (src, a, sr, dst, dr, where, sends, gets) in enumerate(plan):
            copy = pltpu.make_async_remote_copy(
                src_ref=src.at[a, sr, :], dst_ref=dst.at[a, dr, :],
                send_sem=hs.at[c, i], recv_sem=hr.at[c, i],
                device_id=dev(*where), device_id_type=MESH,
            )
            out.append((copy, sends, gets))
        return out

    def when(cond, fn):
        if cond is None:
            fn()
        else:
            pl.when(cond)(fn)

    pl.semaphore_wait(barrier, len(partners))
    for copy, sends, _ in halo(4, ex, 0, 8):
        when(sends, copy.start)

    def send_chunk(c, carry):
        for copy, sends, _ in halo(c, qx, 16 * c, 2 * c):
            when(sends, copy.start)
        return carry

    lax.fori_loop(0, 4, send_chunk, 0)
    swap_theta = pltpu.make_async_remote_copy(
        src_ref=thx, dst_ref=thr, send_sem=xs.at[0], recv_sem=xr.at[0], device_id=pair, device_id_type=MESH
    )
    swap_theta.start()

    for copy, _, gets in halo(4, ex, 0, 8):
        when(gets, copy.wait_recv)
    for rows in ((0, W), (W + 16, 32)):
        pack_edges(ex, 0, rows, 2, rv, lv, 8)
    o = ex[10]
    tabs[0] = o
    tabs[1] = 0.5 * ex[8] * o
    tabs[2] = 0.5 * ex[9] * o
    slot32 = iota((32, 128), 1) // 32

    def spread(x, k):
        y = jnp.where(slot32 == k, x, 0.0)
        y = y + pltpu.roll(y, 32, 1)
        return y + pltpu.roll(y, 64, 1)

    both = strips_of(rv[8], lv[8], rvr[8], lvr[8], 0, 32)
    for side in range(2):
        for k in range(8):
            ftab[side, k] = spread(both[side][k % 2], k // 2)
    both = strips_of(rv[9], lv[9], rvr[9], lvr[9], 0, 32)
    for side in range(2):
        even, odd = both[side]
        o = spread(even, 1)
        stabs[side, 0] = o
        stabs[side, 1] = 0.5 * spread(even, 0) * o
        stabs[side, 2] = 0.5 * spread(odd, 0) * o

    site = obs_index[0]
    site_col = jnp.broadcast_to(site % 128, (16, 128))
    site_row = jnp.broadcast_to(site // 128, (16, 128)) == iota((16, 128), 0)
    lane = iota((16, 128), 1)
    slot16 = lane % 32 < 16
    edge = (lane < W) | (lane >= 128 - W)

    def out_copy(c):
        at = pl.ds(16 * c, 16)
        return pltpu.make_async_copy(fin.at[at], fin_out.at[at], osem.at[c])

    def chunk(c, carry):
        m0 = 16 * c
        for copy, _, gets in halo(c, qx, m0, 2 * c):
            when(gets, copy.wait_recv)
        for rows in ((0, W), (W + 16, 32)):
            pack_edges(qx, m0, rows, 2, rv, lv, 2 * c)
        for p in range(16):
            fos[p] = coefs[3, pl.ds(m0 + p, 1), :] * ex[mode[m0 + p]]

        def keep(p, new):
            fin[m0 + p] = new

        advance(
            lambda p, a, n: qx[m0 + p, a : a + n, :], 16,
            [lambda p, t=t: coefs[t, pl.ds(m0 + p, 1), :] for t in range(3)],
            [lambda p, a, n, t=t: tabs[t, a : a + n, :] for t in range(3)],
            lambda p, a, n: fos[p, a : a + n, :], qs, lqs, es, mask, keep,
        )
        for n in range(2):
            gr = 2 * c + n
            both = strips_of(rv[gr], lv[gr], rvr[gr], lvr[gr], 0, 32)
            for side in range(2):
                for odd in range(2):
                    p = 4 * n + 2 * side + odd
                    qp[p] = both[side][odd]
                    f = None
                    for k in range(4):
                        x = ftab[side, mode[m0 + 8 * n + 2 * k + odd]]
                        f = x if f is None else jnp.where(slot32 == k, x, f)
                    fops[p] = pcoefs[3, odd, pl.ds(gr, 1), :] * f

        def keep_strip(p, new):
            endp[p] = new

        advance(
            lambda p, a, n: qp[p, a : a + n, :], 8,
            [lambda p, t=t: pcoefs[t, p % 2, pl.ds(2 * c + p // 4, 1), :] for t in range(3)],
            [lambda p, a, n, t=t: stabs[(p // 2) % 2, t, a : a + n, :] for t in range(3)],
            lambda p, a, n: fops[p, a : a + n, :], qps, lqps, eps, mask, keep_strip,
        )
        for n in range(2):
            for odd in range(2):
                ends = jnp.where(slot16, endp[4 * n + 2 + odd], endp[4 * n + odd])
                for k in range(4):
                    p = 8 * n + 2 * k + odd
                    moved = pltpu.roll(ends, (112 - 32 * k) % 128, 1)
                    whole = jnp.where(edge, moved, fin[m0 + p])
                    fin[m0 + p] = whole
                    seen = jnp.where(site_row, jnp.take_along_axis(whole, site_col, axis=1), 0.0)
                    oall[e, pl.ds(m0 + p, 1), :] = jnp.sum(seen, axis=0, keepdims=True)
        out_copy(c).start()
        return carry

    lax.fori_loop(0, 4, chunk, 0)

    swap_seen = pltpu.make_async_remote_copy(
        src_ref=oall.at[e], dst_ref=oall.at[e], send_sem=xs.at[1], recv_sem=xr.at[1],
        device_id=pair, device_id_type=MESH,
    )
    swap_seen.start()
    got_seen = pltpu.make_async_remote_copy(
        src_ref=oall.at[e], dst_ref=oall.at[1 - e], send_sem=xs.at[1], recv_sem=xr.at[1],
        device_id=pair, device_id_type=MESH,
    )
    got_seen.wait_recv()
    swap_theta.wait_recv()

    seen = jnp.concatenate([oall[0], oall[1]], axis=0)
    mean = jnp.sum(seen, axis=0, keepdims=True) * (1.0 / 128.0)
    scale = 1.0 / obs_sigma[0]
    anomaly = (seen - mean) * scale
    miss = jnp.broadcast_to((obs_values[0] - mean) * scale, (8, 128))
    dims = (((1,), (1,)), ((), ()))
    gram = lax.dot_general(anomaly, anomaly, dims, precision=HIGHEST, preferred_element_type=F32)
    cvec = lax.dot_general(miss, anomaly, dims, precision=HIGHEST, preferred_element_type=F32)
    gp[...] = gram.reshape(16, 8, 128)
    last = iota((8, 128), 0) == 7
    gp[15] = jnp.where(last, cvec, gram[120:128])

    def spread_out(src, dst, ssem, rsem, count, me, axis):
        outs, ins = [], []
        for d in range(1, count):
            j = lax.rem(me + d, count)
            where = {"gx": z, "gy": g, "ens": e, axis: j}
            outs.append(pltpu.make_async_remote_copy(
                src_ref=src(j), dst_ref=dst.at[me], send_sem=ssem.at[d], recv_sem=rsem.at[me],
                device_id=where, device_id_type=MESH))
            ins.append(pltpu.make_async_remote_copy(
                src_ref=src(j), dst_ref=dst.at[j], send_sem=ssem.at[d], recv_sem=rsem.at[j],
                device_id=where, device_id_type=MESH))
        return outs, ins

    rs[g] = gp[g]
    rs_out, rs_in = spread_out(lambda j: gp.at[j], rs, rss, rsr, ng, g, "gy")
    for c in rs_out:
        c.start()
    for c in rs_in:
        c.wait_recv()
    zs[z] = jnp.sum(rs[...], axis=0)
    z_out, z_in = spread_out(lambda j: zs.at[z], zs, zss, zsr, nz, z, "gx")
    for c in z_out:
        c.start()
    for c in z_in:
        c.wait_recv()
    ag[g] = jnp.sum(zs[...], axis=0)
    ag_out, ag_in = spread_out(lambda j: ag.at[g], ag, ags, agr, ng, g, "gy")
    for c in ag_out:
        c.start()

    th_all = thx[...] + thr[...]
    th_mean = jnp.sum(th_all, axis=1, keepdims=True) * (1.0 / 128.0)
    mat[16] = th_all - th_mean
    for c in ag_in:
        c.wait_recv()

    crow = ag[15, 7:8, :]
    sub, ln = iota((8, 128), 0), iota((8, 128), 1)
    tiles = [ag[t] for t in range(16)]
    tiles[15] = jnp.where(last, 0.0, tiles[15])
    total = tiles[0]
    for t in range(1, 16):
        total = total + tiles[t]
    total = jnp.sum(total, axis=0, keepdims=True)
    tiles[15] = jnp.where(last, -total, tiles[15])
    for t in range(16):
        mat[t] = tiles[t] + jnp.where(ln == sub + 8 * t, 127.0, 0.0)

    front = ln < 8

    def block(k, carry):
        piv = mat[k]
        cols = [jnp.broadcast_to(piv[:, j : j + 1], (8, 128)) for j in range(8)]
        a = [[jnp.broadcast_to(cols[j][i : i + 1, :], (8, 128)) for j in range(8)] for i in range(8)]
        rows = [
            jnp.where(front, jnp.where(ln == i, 1.0, 0.0), jnp.broadcast_to(piv[i : i + 1, :], (8, 128)))
            for i in range(8)
        ]
        for i in range(8):
            inv = 1.0 / a[i][i]
            rows[i] = rows[i] * inv
            for j in range(i + 1, 8):
                a[i][j] = a[i][j] * inv
            for r in range(8):
                if r != i:
                    f = a[r][i]
                    rows[r] = rows[r] - f * rows[i]
                    for j in range(i + 1, 8):
                        a[r][j] = a[r][j] - f * a[i][j]
        rows = [jnp.where(front, -r, r) for r in rows]
        for t in range(17):
            x = mat[t]
            new = jnp.where(front, 0.0, x)
            for i in range(8):
                new = new - jnp.broadcast_to(x[:, i : i + 1], (8, 128)) * rows[i]
            mat[t] = pltpu.roll(new, 120, 1)
        return carry

    lax.fori_loop(0, 16, block, 0)
    zt = mat[16]
    shift = jnp.sum(zt * crow, axis=1, keepdims=True)
    fresh = th_mean + 127.0 * zt + shift
    for p in range(4):
        here = jnp.where(diag, jnp.broadcast_to(fresh[p : p + 1, :], (64, 128)), 0.0)
        theta_out[:, p : p + 1] = jnp.sum(here, axis=1, keepdims=True)

    for copy, sends, _ in halo(4, ex, 0, 8):
        when(sends, copy.wait_send)

    def drain(c, carry):
        for copy, sends, _ in halo(c, qx, 16 * c, 2 * c):
            when(sends, copy.wait_send)
        out_copy(c).wait()
        return carry

    lax.fori_loop(0, 4, drain, 0)
    swap_theta.wait_send()
    swap_seen.wait_send()
    for c in rs_out + z_out + ag_out:
        c.wait_send()


def local(state, u_vel, v_vel, land, forcing, member_mode, theta, obs_index, obs_values, obs_sigma):
    hbm = pl.BlockSpec(memory_space=pl.ANY)
    vmem = pl.BlockSpec(memory_space=pltpu.VMEM)
    dma, v = pltpu.SemaphoreType.DMA, lambda *s: pltpu.VMEM(s, F32)
    return pl.pallas_call(
        kernel,
        out_shape=(jax.ShapeDtypeStruct(state.shape, F32), jax.ShapeDtypeStruct(theta.shape, F32)),
        in_specs=[pl.BlockSpec(memory_space=pltpu.SMEM)] + [hbm] * 5 + [vmem] * 4,
        out_specs=(hbm, vmem),
        scratch_shapes=[
            v(64, 32, 128), v(16, 32, 128), pltpu.VMEM((16, 128), jnp.int32),
            v(10, 32, 128), v(10, 32, 128), v(10, 32, 128), v(10, 32, 128),
            v(32, 128), v(3, 32, 128), v(2, 8, 32, 128), v(2, 3, 32, 128), v(4, 64, 128), v(4, 2, 8, 128),
            v(16, 32, 128), v(16, 32, 128), v(16, 32, 128), v(16, 32, 128),
            v(8, 32, 128), v(8, 32, 128), v(8, 32, 128), v(8, 32, 128), v(8, 32, 128), v(8, 16, 128),
            v(64, 16, 128), v(2, 64, 128), v(8, 128), v(8, 128),
            v(16, 8, 128), v(16, 8, 128), v(8, 8, 128), v(16, 8, 128), v(17, 8, 128),
            dma((5,)), dma((4,)), dma((5, 8)), dma((5, 8)), dma((2,)), dma((2,)),
            dma((16,)), dma((16,)), dma((8,)), dma((8,)), dma((16,)), dma((16,)),
        ],
        compiler_params=pltpu.CompilerParams(collective_id=0, has_side_effects=True),
    )(member_mode, state, u_vel, v_vel, land, forcing, theta, obs_index, obs_values, obs_sigma)


def solution(mesh):
    in_specs = (
        P("ens", "gy", "gx"), P("gy", "gx"), P("gy", "gx"), P("gy", "gx"), P(None, "gy", "gx"),
        P("ens"), P("ens", None), P("gy", "gx", None), P("gy", "gx", None), P("gy", "gx", None),
    )
    out_specs = (P("ens", "gy", "gx"), P("ens", None))

    def run(state, u_vel, v_vel, land, forcing, member_mode, theta, obs_index, obs_values, obs_sigma):
        flat = [a.reshape(a.shape[1:]) for a in (obs_index, obs_values, obs_sigma)]
        return local(state, u_vel, v_vel, land, forcing, member_mode, theta, *flat)

    return jax.shard_map(run, mesh=mesh, in_specs=in_specs, out_specs=out_specs, check_vma=False)
```

time: 185 us -> 63.3 us (0.34)
  waiting for transfers between devices: 76.6 us -> 0 us
  Pallas kernels: 0 us -> 57.6 us
  starting transfers between devices: 44.7 us -> 0 us
  other arithmetic: 35 us -> 0 us
  blocking collectives: 18.2 us -> 0 us
  matrix products: 3.42 us -> 0 us
    pallas_call x0 -> x1, Pallas kernels: none -> 57.6 us  [local(): pl.pallas_call(kernel, out_shape=(jax.ShapeDtypeStruct(state.shape, F32),...]
    ppermute x16 -> x0, waiting for transfers between devices: 55.9 us -> none  [the longest x8 43.6 us: with_halo(): lax.ppermute(lax.slice_in_dim(block, block.shape[dim] - width, None, axis...]
    ppermute x16 -> x0, starting transfers between devices: 31.2 us -> none  [the longest x8 21.2 us: with_halo(): lax.ppermute(lax.slice_in_dim(block, block.shape[dim] - width, None, axis...]
    another operation x5 -> x0, other arithmetic: 22.9 us -> none  [the longest x3 12.4 us: local(): factor = jnp.linalg.cholesky(system)]
    all_to_all x2 -> x0, waiting for transfers between devices: 20.7 us -> none  [the longest x1 11 us: copy_for_each(): return lax.all_to_all(copies, axis, split_axis=0, concat_axis=0, tiled=True)]
    all_to_all x2 -> x0, blocking collectives: 14.4 us -> none  [the longest x1 7.95 us: summed_on_arrival(): lax.all_to_all(pieces, axis, split_axis=0, concat_axis=0, tiled=True)]
    all_to_all x2 -> x0, starting transfers between devices: 13.5 us -> none  [the longest x1 8.86 us: sum_by_axis(): lax.all_to_all(nearer, far, split_axis=0, concat_axis=0, tiled=True)]
    mul x13 -> x0, other arithmetic: 11.2 us -> none  [the longest x4 5.2 us: local(): lap_wide = laplace(extended) * wall_one]
  transfers between devices with their start and end apart: 18 -> 0, of which waited for: 16 -> 0; matrix products, arithmetic and copies ran while one was open for 1% -> 0% of each run, Pallas kernels for 0% -> 0%
where the time goes in v1:
time: 63.3 us; the launch traced here: 63 us
  Pallas kernels  57.6 us (91%)
  local copies, waits for them, and re-layouts  4.66 us (7%)
  between operations  0.65 us (1%)
    pallas_call x1, Pallas kernels, local(): pl.pallas_call(kernel, out_shape=(jax.ShapeDtypeStruct(state.shape, F32),...  57.6 us
    unnamed x4, local copies, waits for them, and re-layouts  3.25 us
    pallas_call x1, local copies, waits for them, and re-layouts, local(): pl.pallas_call(kernel, out_shape=(jax.ShapeDtypeStruct(state.shape, F32),...  1.41 us

profile of v1, /device:TPU:1, one launch (start us, length us, event | category | flops | bytes accessed | tf_op | source)
XLA Modules:
  0.0 63.0 jit_solution(16425277951726839722)
XLA Ops:
  0.6 0.0 copy-start
  0.6 0.7 %copy-done = f32[64,4]{0,1:T(4,128)S(1)} copy-done((f32[64,4]{0,1:T(4,128)S(1)}, f32[64,4]{0,1:T(4,128)}, u32[]{:S(2)}) %copy-start) | copy-done | bytes 1048
  1.3 0.7 %copy.12.theta = f32[64,4]{1,0:T(8,128)} copy(f32[64,4]{0,1:T(4,128)S(1)} %copy-done) | data formatting | bytes 2048 | tf_op args[6]
  2.0 57.6 %shard_map.113 = (f32[64,16,128]{2,1,0:T(8,128)}, f32[64,4]{1,0:T(8,128)}) custom-call(s32[64]{0:T(128)} %mode.1, f32[64,16,128]{2,1,0:T(8,128)} %state.1, f32[16,128]{1,0:T(8,128)} %u_vel.1, f32[16,128]{1,0:T(8,128)} %v_vel.1, s32[16,128]{1,0:T(8,128)} %land.1, f32[8,16,128]{2,1,0:T(8,128)} %forcing.1, f32[64,4]{1,0:T(8,128)} %copy.12.theta, ...), custom_call_target="tpu_custom_call" | custom-call | tf_op jit(solution)/shard_map/pallas_call | solution.py:432
  59.7 1.4 %copy.13 = f32[64,4]{0,1:T(4,128)} copy(f32[64,4]{1,0:T(8,128)} %get-tuple-element.3) | data formatting | bytes 2048 | tf_op jit(solution)/shard_map/pallas_call | solution.py:432
  61.1 1.9 %copy.15 = f32[64,16,128]{2,1,0:T(8,128)} copy(f32[64,16,128]{2,1,0:T(8,128)} %get-tuple-element.6) | data formatting | bytes 1048576
Async XLA Ops:
  0.6 0.7 %copy-start = (f32[64,4]{0,1:T(4,128)S(1)}, f32[64,4]{0,1:T(4,128)}, u32[]{:S(2)}) copy-start(f32[64,4]{0,1:T(4,128)} %param.16) | copy-start | bytes 3076

commit v2 on v1

--- a/solution.py
+++ b/solution.py
@@ -79,12 +79,12 @@
 
 
 def kernel(
-    mode, state, u_vel, v_vel, land, forcing, theta, obs_index, obs_values, obs_sigma,
+    mode_in, state, u_vel, v_vel, land, forcing, theta, obs_index, obs_values, obs_sigma,
     fin_out, theta_out,
     qx, ex, landb, rv, lv, rvr, lvr, mask, tabs, ftab, stabs, coefs, pcoefs,
     qs, lqs, es, fos, qp, qps, lqps, eps, fops, endp, fin, oall, thx, thr,
     gp, rs, zs, ag, mat,
-    lsem, osem, hs, hr, xs, xr, rss, rsr, zss, zsr, ags, agr,
+    thl, oix, ova, osg, mode, lsem, osem, hs, hr, xs, xr, rss, rsr, zss, zsr, ags, agr,
 ):
     z, g, e = lax.axis_index("gx"), lax.axis_index("gy"), lax.axis_index("ens")
     nz, ng = 8, 16
@@ -107,24 +107,39 @@
         pltpu.make_async_copy(u_vel, ex.at[8, own, :], lsem.at[2]),
         pltpu.make_async_copy(v_vel, ex.at[9, own, :], lsem.at[3]),
         pltpu.make_async_copy(land, landb, lsem.at[4]),
+        pltpu.make_async_copy(theta, thl, lsem.at[5]),
+        pltpu.make_async_copy(obs_index, oix, lsem.at[6]),
+        pltpu.make_async_copy(obs_values, ova, lsem.at[7]),
+        pltpu.make_async_copy(obs_sigma, osg, lsem.at[8]),
+        pltpu.make_async_copy(mode_in, mode, lsem.at[9]),
     ]
-    for c in loads:
+    for c in (loads[5], *loads[:5], *loads[6:]):
         c.start()
-
-    lane64 = iota((64, 128), 1)
-    diag = lane64 == iota((64, 128), 0) + 64 * e
-    tt = theta[...]
+    loads[5].wait()
+
+    same = iota((64, 64), 0) == iota((64, 64), 1)
+
+    def across(row):
+        col = jnp.sum(jnp.where(same, jnp.broadcast_to(row, (64, 64)), 0.0), axis=1, keepdims=True)
+        return jnp.broadcast_to(col, (64, 128))
+
+    tt = thl[...]
     th = jnp.tanh(tt)
-    spread4 = [jnp.broadcast_to(th[:, p : p + 1], (64, 128)) for p in range(3)]
-    raw4 = [jnp.broadcast_to(tt[:, p : p + 1], (64, 128)) for p in range(4)]
-    hyper = 0.005 * (1.0 + 0.5 * spread4[1])
-    coefs[0] = 1.0 - 0.05 * (1.0 + 0.5 * spread4[2])
-    coefs[1] = 0.05 * (1.0 + 0.5 * spread4[0]) + 4.0 * hyper
-    coefs[2] = hyper
-    coefs[3] = raw4[3]
+    hyper = 0.005 * (1.0 + 0.5 * th[1:2])
+    coefs[0] = across(1.0 - 0.05 * (1.0 + 0.5 * th[2:3]))
+    coefs[1] = across(0.05 * (1.0 + 0.5 * th[0:1]) + 4.0 * hyper)
+    coefs[2] = across(hyper)
+    coefs[3] = across(tt[3:4])
     thx[...] = jnp.zeros((8, 128), F32)
-    for p in range(4):
-        thx[p : p + 1, :] = jnp.sum(jnp.where(diag, raw4[p], 0.0), axis=0, keepdims=True)
+
+    @pl.when(e == 0)
+    def _():
+        thx[0:4, 0:64] = thl[...]
+
+    @pl.when(e == 1)
+    def _():
+        thx[0:4, 64:128] = thl[...]
+
     slot8 = iota((8, 128), 1) // 32
     for t in range(4):
         for odd in range(2):
@@ -137,7 +152,7 @@
     no_wall = (jnp.logical_or(row32 >= W, up_ok)) & (jnp.logical_or(row32 < W + 16, down_ok))
     mask[...] = no_wall.astype(F32)
 
-    for c in loads[1:]:
+    for c in loads[1:5] + loads[6:]:
         c.wait()
     ex[10, W : W + 16, :] = (1 - landb[...]).astype(F32)
     ex[11:16, W : W + 16, :] = jnp.zeros((5, 16, 128), F32)
@@ -233,7 +248,7 @@
         stabs[side, 1] = 0.5 * spread(even, 0) * o
         stabs[side, 2] = 0.5 * spread(odd, 0) * o
 
-    site = obs_index[0]
+    site = oix[...]
     site_col = jnp.broadcast_to(site % 128, (16, 128))
     site_row = jnp.broadcast_to(site // 128, (16, 128)) == iota((16, 128), 0)
     lane = iota((16, 128), 1)
@@ -313,9 +328,9 @@
 
     seen = jnp.concatenate([oall[0], oall[1]], axis=0)
     mean = jnp.sum(seen, axis=0, keepdims=True) * (1.0 / 128.0)
-    scale = 1.0 / obs_sigma[0]
+    scale = 1.0 / osg[...]
     anomaly = (seen - mean) * scale
-    miss = jnp.broadcast_to((obs_values[0] - mean) * scale, (8, 128))
+    miss = jnp.broadcast_to((ova[...] - mean) * scale, (8, 128))
     dims = (((1,), (1,)), ((), ()))
     gram = lax.dot_general(anomaly, anomaly, dims, precision=HIGHEST, preferred_element_type=F32)
     cvec = lax.dot_general(miss, anomaly, dims, precision=HIGHEST, preferred_element_type=F32)
@@ -371,43 +386,38 @@
     for t in range(16):
         mat[t] = tiles[t] + jnp.where(ln == sub + 8 * t, 127.0, 0.0)
 
-    front = ln < 8
-
-    def block(k, carry):
+    for k in range(16):
+        base = 8 * k
+        front = (ln >= base) & (ln < base + 8)
         piv = mat[k]
-        cols = [jnp.broadcast_to(piv[:, j : j + 1], (8, 128)) for j in range(8)]
-        a = [[jnp.broadcast_to(cols[j][i : i + 1, :], (8, 128)) for j in range(8)] for i in range(8)]
-        rows = [
-            jnp.where(front, jnp.where(ln == i, 1.0, 0.0), jnp.broadcast_to(piv[i : i + 1, :], (8, 128)))
-            for i in range(8)
-        ]
+        cols = [jnp.broadcast_to(piv[:, base + j : base + j + 1], (8, 128)) for j in range(8)]
+        row = jnp.where(front, jnp.where(ln == sub + base, 1.0, 0.0), piv)
         for i in range(8):
-            inv = 1.0 / a[i][i]
-            rows[i] = rows[i] * inv
+            at = [jnp.broadcast_to(cols[j][i : i + 1, :], (8, 128)) for j in range(i, 8)]
+            inv = 1.0 / at[0]
+            mine = sub == i
+            step = jnp.where(mine, -1.0, cols[i])
+            row = jnp.where(mine, 0.0, row) - step * (jnp.broadcast_to(row[i : i + 1, :], (8, 128)) * inv)
             for j in range(i + 1, 8):
-                a[i][j] = a[i][j] * inv
-            for r in range(8):
-                if r != i:
-                    f = a[r][i]
-                    rows[r] = rows[r] - f * rows[i]
-                    for j in range(i + 1, 8):
-                        a[r][j] = a[r][j] - f * a[i][j]
-        rows = [jnp.where(front, -r, r) for r in rows]
-        for t in range(17):
+                cols[j] = jnp.where(mine, 0.0, cols[j]) - step * (at[j - i] * inv)
+        row = jnp.where(front, -row, row)
+        rows = [jnp.broadcast_to(row[i : i + 1, :], (8, 128)) for i in range(8)]
+        for t in range(k + 1, 17):
             x = mat[t]
             new = jnp.where(front, 0.0, x)
             for i in range(8):
-                new = new - jnp.broadcast_to(x[:, i : i + 1], (8, 128)) * rows[i]
-            mat[t] = pltpu.roll(new, 120, 1)
-        return carry
-
-    lax.fori_loop(0, 16, block, 0)
+                new = new - jnp.broadcast_to(x[:, base + i : base + i + 1], (8, 128)) * rows[i]
+            mat[t] = new
     zt = mat[16]
     shift = jnp.sum(zt * crow, axis=1, keepdims=True)
     fresh = th_mean + 127.0 * zt + shift
-    for p in range(4):
-        here = jnp.where(diag, jnp.broadcast_to(fresh[p : p + 1, :], (64, 128)), 0.0)
-        theta_out[:, p : p + 1] = jnp.sum(here, axis=1, keepdims=True)
+    @pl.when(e == 0)
+    def _():
+        theta_out[...] = fresh[0:4, 0:64]
+
+    @pl.when(e == 1)
+    def _():
+        theta_out[...] = fresh[0:4, 64:128]
 
     for copy, sends, _ in halo(4, ex, 0, 8):
         when(sends, copy.wait_send)
@@ -432,7 +442,7 @@
     return pl.pallas_call(
         kernel,
         out_shape=(jax.ShapeDtypeStruct(state.shape, F32), jax.ShapeDtypeStruct(theta.shape, F32)),
-        in_specs=[pl.BlockSpec(memory_space=pltpu.SMEM)] + [hbm] * 5 + [vmem] * 4,
+        in_specs=[hbm] * 10,
         out_specs=(hbm, vmem),
         scratch_shapes=[
             v(64, 32, 128), v(16, 32, 128), pltpu.VMEM((16, 128), jnp.int32),
@@ -442,7 +452,8 @@
             v(8, 32, 128), v(8, 32, 128), v(8, 32, 128), v(8, 32, 128), v(8, 32, 128), v(8, 16, 128),
             v(64, 16, 128), v(2, 64, 128), v(8, 128), v(8, 128),
             v(16, 8, 128), v(16, 8, 128), v(8, 8, 128), v(16, 8, 128), v(17, 8, 128),
-            dma((5,)), dma((4,)), dma((5, 8)), dma((5, 8)), dma((2,)), dma((2,)),
+            v(4, 64), pltpu.VMEM((1, 128), jnp.int32), v(1, 128), v(1, 128), pltpu.SMEM((64,), jnp.int32),
+            dma((10,)), dma((4,)), dma((5, 8)), dma((5, 8)), dma((2,)), dma((2,)),
             dma((16,)), dma((16,)), dma((8,)), dma((8,)), dma((16,)), dma((16,)),
         ],
         compiler_params=pltpu.CompilerParams(collective_id=0, has_side_effects=True),
@@ -458,6 +469,7 @@
 
     def run(state, u_vel, v_vel, land, forcing, member_mode, theta, obs_index, obs_values, obs_sigma):
         flat = [a.reshape(a.shape[1:]) for a in (obs_index, obs_values, obs_sigma)]
-        return local(state, u_vel, v_vel, land, forcing, member_mode, theta, *flat)
+        fin, new = local(state, u_vel, v_vel, land, forcing, member_mode, theta.T, *flat)
+        return fin, new.T
 
     return jax.shard_map(run, mesh=mesh, in_specs=in_specs, out_specs=out_specs, check_vma=False)

time: 63.3 us -> 52.9 us (0.84)
  Pallas kernels: 57.6 us -> 49.7 us
  local copies, waits for them, and re-layouts: 4.66 us -> 2.45 us
    pallas_call x1, Pallas kernels: 57.6 us -> 49.7 us  [local(): pl.pallas_call(kernel, out_shape=(jax.ShapeDtypeStruct(state.shape, F32),...]
    pallas_call x1 -> x0, local copies, waits for them, and re-layouts: 1.41 us -> none  [local(): pl.pallas_call(kernel, out_shape=(jax.ShapeDtypeStruct(state.shape, F32),...]
    unnamed x4, local copies, waits for them, and re-layouts: 3.25 us -> 2.45 us
where the time goes in v2:
time: 52.9 us; the launch traced here: 52.8 us
  Pallas kernels  49.7 us (94%)
  local copies, waits for them, and re-layouts  2.45 us (5%)
  between operations  0.65 us (1%)
    pallas_call x1, Pallas kernels, local(): pl.pallas_call(kernel, out_shape=(jax.ShapeDtypeStruct(state.shape, F32),...  49.7 us
    unnamed x4, local copies, waits for them, and re-layouts  2.45 us

profile of v2, /device:TPU:1, one launch (start us, length us, event | category | flops | bytes accessed | tf_op | source)
XLA Modules:
  0.0 52.8 jit_solution(11905129936918290983)
XLA Ops:
  0.6 49.7 %shard_map.113 = (f32[64,16,128]{2,1,0:T(8,128)}, f32[4,64]{1,0:T(4,128)}) custom-call(s32[64]{0:T(128)} %mode_in.1, f32[64,16,128]{2,1,0:T(8,128)} %state.1, f32[16,128]{1,0:T(8,128)} %u_vel.1, f32[16,128]{1,0:T(8,128)} %v_vel.1, s32[16,128]{1,0:T(8,128)} %land.1, f32[8,16,128]{2,1,0:T(8,128)} %forcing.1, f32[4,64]{1,0:T(4,128)} %bitcast.5, ...), custom_call_target="tpu_custom_call" | custom-call | tf_op jit(solution)/shard_map/pallas_call | solution.py:442
  50.3 0.0 copy-start
  50.4 1.9 %copy.14 = f32[64,16,128]{2,1,0:T(8,128)} copy(f32[64,16,128]{2,1,0:T(8,128)} %get-tuple-element.8) | data formatting | bytes 1048576
  52.2 0.0 copy-done
  52.2 0.6 %copy.15 = f32[64,4]{0,1:T(4,128)} copy(f32[64,4]{0,1:T(4,128)S(1)} %bitcast.6) | data formatting | bytes 2048
Async XLA Ops:
  50.3 1.9 %copy-start = (f32[4,64]{1,0:T(4,128)S(1)}, f32[4,64]{1,0:T(4,128)}, u32[]{:S(2)}) copy-start(f32[4,64]{1,0:T(4,128)} %get-tuple-element.5) | copy-start | bytes 3076

commit v3 on v2

--- a/solution.py
+++ b/solution.py
@@ -10,7 +10,7 @@
 MESH = pl.DeviceIdType.MESH
 F32 = jnp.float32
 HIGHEST = lax.Precision.HIGHEST
-CHUNK = 16
+AHEAD = 4
 
 
 def iota(shape, dim):
@@ -84,7 +84,7 @@
     qx, ex, landb, rv, lv, rvr, lvr, mask, tabs, ftab, stabs, coefs, pcoefs,
     qs, lqs, es, fos, qp, qps, lqps, eps, fops, endp, fin, oall, thx, thr,
     gp, rs, zs, ag, mat,
-    thl, oix, ova, osg, mode, lsem, osem, hs, hr, xs, xr, rss, rsr, zss, zsr, ags, agr,
+    pick, thl, oix, ova, osg, mode, lsem, osem, hs, hr, xs, xr, rss, rsr, zss, zsr, ags, agr,
 ):
     z, g, e = lax.axis_index("gx"), lax.axis_index("gy"), lax.axis_index("ens")
     nz, ng = 8, 16
@@ -94,9 +94,14 @@
         return {"gx": lax.rem(z + dz + nz, nz), "gy": lax.rem(g + dg + ng, ng), "ens": e}
 
     pair = {"gx": z, "gy": g, "ens": 1 - e}
+    near = lax.rem(g // 8 + e, 2)
+
+    def tile_holder(j):
+        return {"gx": z, "gy": j, "ens": lax.rem(j // 8 + near, 2)}
+
     barrier = pltpu.get_barrier_semaphore()
-    partners = [dev(0, d) for d in range(1, ng)] + [dev(d, 0) for d in range(1, nz)] + [pair]
-    partners += [dev(a, b) for a in (-1, 1) for b in (-1, 1)]
+    partners = [tile_holder(lax.rem(g + d, ng)) for d in range(1, ng)] + [dev(d, 0) for d in range(1, nz)] + [pair]
+    partners += [dev(a, b) for a in (-1, 0, 1) for b in (-1, 1)]
     for where in partners:
         pl.semaphore_signal(barrier, inc=1, device_id=where, device_id_type=MESH)
 
@@ -113,49 +118,8 @@
         pltpu.make_async_copy(obs_sigma, osg, lsem.at[8]),
         pltpu.make_async_copy(mode_in, mode, lsem.at[9]),
     ]
-    for c in (loads[5], *loads[:5], *loads[6:]):
+    for c in loads:
         c.start()
-    loads[5].wait()
-
-    same = iota((64, 64), 0) == iota((64, 64), 1)
-
-    def across(row):
-        col = jnp.sum(jnp.where(same, jnp.broadcast_to(row, (64, 64)), 0.0), axis=1, keepdims=True)
-        return jnp.broadcast_to(col, (64, 128))
-
-    tt = thl[...]
-    th = jnp.tanh(tt)
-    hyper = 0.005 * (1.0 + 0.5 * th[1:2])
-    coefs[0] = across(1.0 - 0.05 * (1.0 + 0.5 * th[2:3]))
-    coefs[1] = across(0.05 * (1.0 + 0.5 * th[0:1]) + 4.0 * hyper)
-    coefs[2] = across(hyper)
-    coefs[3] = across(tt[3:4])
-    thx[...] = jnp.zeros((8, 128), F32)
-
-    @pl.when(e == 0)
-    def _():
-        thx[0:4, 0:64] = thl[...]
-
-    @pl.when(e == 1)
-    def _():
-        thx[0:4, 64:128] = thl[...]
-
-    slot8 = iota((8, 128), 1) // 32
-    for t in range(4):
-        for odd in range(2):
-            acc = None
-            for k in range(4):
-                x = coefs[t, pl.ds(odd + 2 * k, 8, stride=8), :]
-                acc = x if acc is None else jnp.where(slot8 == k, x, acc)
-            pcoefs[t, odd] = acc
-    row32 = iota((32, 128), 0)
-    no_wall = (jnp.logical_or(row32 >= W, up_ok)) & (jnp.logical_or(row32 < W + 16, down_ok))
-    mask[...] = no_wall.astype(F32)
-
-    for c in loads[1:5] + loads[6:]:
-        c.wait()
-    ex[10, W : W + 16, :] = (1 - landb[...]).astype(F32)
-    ex[11:16, W : W + 16, :] = jnp.zeros((5, 16, 128), F32)
 
     @pl.when(jnp.logical_not(up_ok))
     def _():
@@ -166,15 +130,6 @@
     def _():
         for ref in (qx, ex, rvr, lvr):
             ref[:, W + 16 :, :] = jnp.zeros((ref.shape[0], W, 128), F32)
-
-    pack_edges(ex, 0, (W, W + 16), 2, rv, lv, 8)
-    loads[0].wait()
-
-    def pack_own(c, carry):
-        pack_edges(qx, 16 * c, (W, W + 16), 2, rv, lv, 2 * c)
-        return carry
-
-    lax.fori_loop(0, 4, pack_own, 0)
 
     top, bottom, low, high = pl.ds(W, W), pl.ds(16, W), pl.ds(0, W), pl.ds(W + 16, W)
 
@@ -206,16 +161,69 @@
         else:
             pl.when(cond)(fn)
 
+    def send(copies):
+        for copy, sends, _ in copies:
+            when(sends, copy.start)
+
+    for c in loads[1:5]:
+        c.wait()
+    ex[10, W : W + 16, :] = (1 - landb[...]).astype(F32)
+    ex[11:16, W : W + 16, :] = jnp.zeros((5, 16, 128), F32)
+    loads[0].wait()
+    pack_edges(ex, 0, (W, W + 16), 2, rv, lv, 8)
+
+    def pack_own(c, carry):
+        pack_edges(qx, 16 * c, (W, W + 16), 2, rv, lv, 2 * c)
+        return carry
+
+    lax.fori_loop(0, 4, pack_own, 0)
     pl.semaphore_wait(barrier, len(partners))
-    for copy, sends, _ in halo(4, ex, 0, 8):
-        when(sends, copy.start)
+    send(halo(4, ex, 0, 8))
 
     def send_chunk(c, carry):
-        for copy, sends, _ in halo(c, qx, 16 * c, 2 * c):
-            when(sends, copy.start)
+        send(halo(c, qx, 16 * c, 2 * c))
         return carry
 
-    lax.fori_loop(0, 4, send_chunk, 0)
+    lax.fori_loop(0, AHEAD, send_chunk, 0)
+
+    for c in loads[5:]:
+        c.wait()
+    same = iota((64, 64), 0) == iota((64, 64), 1)
+
+    def across(row):
+        col = jnp.sum(jnp.where(same, jnp.broadcast_to(row, (64, 64)), 0.0), axis=1, keepdims=True)
+        return jnp.broadcast_to(col, (64, 128))
+
+    tt = thl[...]
+    th = jnp.tanh(tt)
+    hyper = 0.005 * (1.0 + 0.5 * th[1:2])
+    coefs[0] = across(1.0 - 0.05 * (1.0 + 0.5 * th[2:3]))
+    coefs[1] = across(0.05 * (1.0 + 0.5 * th[0:1]) + 4.0 * hyper)
+    coefs[2] = across(hyper)
+    coefs[3] = across(tt[3:4])
+    thx[...] = jnp.zeros((8, 128), F32)
+
+    @pl.when(e == 0)
+    def _():
+        thx[0:4, 0:64] = thl[...]
+
+    @pl.when(e == 1)
+    def _():
+        thx[0:4, 64:128] = thl[...]
+
+    slot8 = iota((8, 128), 1) // 32
+    for t in range(4):
+        for odd in range(2):
+            acc = None
+            for k in range(4):
+                x = coefs[t, pl.ds(odd + 2 * k, 8, stride=8), :]
+                acc = x if acc is None else jnp.where(slot8 == k, x, acc)
+            pcoefs[t, odd] = acc
+    row32 = iota((32, 128), 0)
+    no_wall = (jnp.logical_or(row32 >= W, up_ok)) & (jnp.logical_or(row32 < W + 16, down_ok))
+    mask[...] = no_wall.astype(F32)
+
+
     swap_theta = pltpu.make_async_remote_copy(
         src_ref=thx, dst_ref=thr, send_sem=xs.at[0], recv_sem=xr.at[0], device_id=pair, device_id_type=MESH
     )
@@ -249,20 +257,25 @@
         stabs[side, 2] = 0.5 * spread(odd, 0) * o
 
     site = oix[...]
-    site_col = jnp.broadcast_to(site % 128, (16, 128))
+    col_pick = jnp.broadcast_to(site % 128, (128, 128)) == iota((128, 128), 0)
+    for n in range(3):
+        pick[128 * n : 128 * n + 128, :] = col_pick.astype(F32).astype(jnp.bfloat16)
     site_row = jnp.broadcast_to(site // 128, (16, 128)) == iota((16, 128), 0)
     lane = iota((16, 128), 1)
     slot16 = lane % 32 < 16
     edge = (lane < W) | (lane >= 128 - W)
 
-    def out_copy(c):
-        at = pl.ds(16 * c, 16)
-        return pltpu.make_async_copy(fin.at[at], fin_out.at[at], osem.at[c])
+    out_copy = pltpu.make_async_copy(fin, fin_out, osem.at[0])
 
     def chunk(c, carry):
         m0 = 16 * c
         for copy, _, gets in halo(c, qx, m0, 2 * c):
             when(gets, copy.wait_recv)
+
+        @pl.when(c + AHEAD < 4)
+        def _():
+            send_chunk(c + AHEAD, 0)
+
         for rows in ((0, W), (W + 16, 32)):
             pack_edges(qx, m0, rows, 2, rv, lv, 2 * c)
         for p in range(16):
@@ -291,7 +304,7 @@
                     fops[p] = pcoefs[3, odd, pl.ds(gr, 1), :] * f
 
         def keep_strip(p, new):
-            endp[p] = new
+            endp[8 * c + p] = new
 
         advance(
             lambda p, a, n: qp[p, a : a + n, :], 8,
@@ -299,20 +312,27 @@
             [lambda p, a, n, t=t: stabs[(p // 2) % 2, t, a : a + n, :] for t in range(3)],
             lambda p, a, n: fops[p, a : a + n, :], qps, lqps, eps, mask, keep_strip,
         )
-        for n in range(2):
-            for odd in range(2):
-                ends = jnp.where(slot16, endp[4 * n + 2 + odd], endp[4 * n + odd])
-                for k in range(4):
-                    p = 8 * n + 2 * k + odd
-                    moved = pltpu.roll(ends, (112 - 32 * k) % 128, 1)
-                    whole = jnp.where(edge, moved, fin[m0 + p])
-                    fin[m0 + p] = whole
-                    seen = jnp.where(site_row, jnp.take_along_axis(whole, site_col, axis=1), 0.0)
-                    oall[e, pl.ds(m0 + p, 1), :] = jnp.sum(seen, axis=0, keepdims=True)
-        out_copy(c).start()
         return carry
 
     lax.fori_loop(0, 4, chunk, 0)
+
+    for c in range(4):
+        for q in range(4):
+            n, odd = q // 2, q % 2
+            ends = jnp.where(slot16, endp[8 * c + 4 * n + 2 + odd], endp[8 * c + 4 * n + odd])
+            for k in range(4):
+                p = 16 * c + 8 * n + 2 * k + odd
+                fin[p] = jnp.where(edge, pltpu.roll(ends, (112 - 32 * k) % 128, 1), fin[p])
+    out_copy.start()
+    for c in range(4):
+        x = fin[16 * c : 16 * c + 16].reshape(256, 128)
+        part, parts = x, []
+        for _ in range(3):
+            parts.append(part.astype(jnp.bfloat16))
+            part = part - parts[-1].astype(F32)
+        at_col = jnp.dot(jnp.concatenate(parts, axis=1), pick[...], preferred_element_type=F32)
+        seen = jnp.where(site_row[None], at_col.reshape(16, 16, 128), 0.0)
+        oall[e, 16 * c : 16 * c + 16, :] = jnp.sum(seen, axis=1)
 
     swap_seen = pltpu.make_async_remote_copy(
         src_ref=oall.at[e], dst_ref=oall.at[e], send_sem=xs.at[1], recv_sem=xr.at[1],
@@ -338,11 +358,11 @@
     last = iota((8, 128), 0) == 7
     gp[15] = jnp.where(last, cvec, gram[120:128])
 
-    def spread_out(src, dst, ssem, rsem, count, me, axis):
+    def spread_out(src, dst, ssem, rsem, count, me, place):
         outs, ins = [], []
         for d in range(1, count):
             j = lax.rem(me + d, count)
-            where = {"gx": z, "gy": g, "ens": e, axis: j}
+            where = place(j)
             outs.append(pltpu.make_async_remote_copy(
                 src_ref=src(j), dst_ref=dst.at[me], send_sem=ssem.at[d], recv_sem=rsem.at[me],
                 device_id=where, device_id_type=MESH))
@@ -352,19 +372,19 @@
         return outs, ins
 
     rs[g] = gp[g]
-    rs_out, rs_in = spread_out(lambda j: gp.at[j], rs, rss, rsr, ng, g, "gy")
+    rs_out, rs_in = spread_out(lambda j: gp.at[j], rs, rss, rsr, ng, g, tile_holder)
     for c in rs_out:
         c.start()
     for c in rs_in:
         c.wait_recv()
     zs[z] = jnp.sum(rs[...], axis=0)
-    z_out, z_in = spread_out(lambda j: zs.at[z], zs, zss, zsr, nz, z, "gx")
+    z_out, z_in = spread_out(lambda j: zs.at[z], zs, zss, zsr, nz, z, lambda j: {"gx": j, "gy": g, "ens": e})
     for c in z_out:
         c.start()
     for c in z_in:
         c.wait_recv()
     ag[g] = jnp.sum(zs[...], axis=0)
-    ag_out, ag_in = spread_out(lambda j: ag.at[g], ag, ags, agr, ng, g, "gy")
+    ag_out, ag_in = spread_out(lambda j: ag.at[g], ag, ags, agr, ng, g, tile_holder)
     for c in ag_out:
         c.start()
 
@@ -386,28 +406,42 @@
     for t in range(16):
         mat[t] = tiles[t] + jnp.where(ln == sub + 8 * t, 127.0, 0.0)
 
+    def lanes_of(x, base):
+        return [jnp.broadcast_to(x[:, base + j : base + j + 1], (8, 128)) for j in range(8)]
+
+    def row_of(x, i):
+        return jnp.broadcast_to(x[i : i + 1, :], (8, 128))
+
+    cols = lanes_of(tiles[0] + jnp.where(ln == sub, 127.0, 0.0), 0)
     for k in range(16):
         base = 8 * k
         front = (ln >= base) & (ln < base + 8)
         piv = mat[k]
-        cols = [jnp.broadcast_to(piv[:, base + j : base + j + 1], (8, 128)) for j in range(8)]
+        ahead = lanes_of(piv, base + 8) if k < 15 else []
         row = jnp.where(front, jnp.where(ln == sub + base, 1.0, 0.0), piv)
         for i in range(8):
-            at = [jnp.broadcast_to(cols[j][i : i + 1, :], (8, 128)) for j in range(i, 8)]
+            at = [row_of(cols[j], i) for j in range(i, 8)]
             inv = 1.0 / at[0]
             mine = sub == i
             step = jnp.where(mine, -1.0, cols[i])
-            row = jnp.where(mine, 0.0, row) - step * (jnp.broadcast_to(row[i : i + 1, :], (8, 128)) * inv)
+            row = jnp.where(mine, 0.0, row) - step * (row_of(row, i) * inv)
             for j in range(i + 1, 8):
                 cols[j] = jnp.where(mine, 0.0, cols[j]) - step * (at[j - i] * inv)
+            ahead = [jnp.where(mine, 0.0, x) - step * (row_of(x, i) * inv) for x in ahead]
         row = jnp.where(front, -row, row)
-        rows = [jnp.broadcast_to(row[i : i + 1, :], (8, 128)) for i in range(8)]
+        rows = [row_of(row, i) for i in range(8)]
         for t in range(k + 1, 17):
             x = mat[t]
+            by = lanes_of(x, base)
             new = jnp.where(front, 0.0, x)
             for i in range(8):
-                new = new - jnp.broadcast_to(x[:, base + i : base + i + 1], (8, 128)) * rows[i]
+                new = new - by[i] * rows[i]
             mat[t] = new
+            if t == k + 1 and k < 15:
+                cols = lanes_of(x, base + 8)
+                for j in range(8):
+                    for i in range(8):
+                        cols[j] = cols[j] - by[i] * row_of(ahead[j], i)
     zt = mat[16]
     shift = jnp.sum(zt * crow, axis=1, keepdims=True)
     fresh = th_mean + 127.0 * zt + shift
@@ -425,10 +459,10 @@
     def drain(c, carry):
         for copy, sends, _ in halo(c, qx, 16 * c, 2 * c):
             when(sends, copy.wait_send)
-        out_copy(c).wait()
         return carry
 
     lax.fori_loop(0, 4, drain, 0)
+    out_copy.wait()
     swap_theta.wait_send()
     swap_seen.wait_send()
     for c in rs_out + z_out + ag_out:
@@ -449,11 +483,11 @@
             v(10, 32, 128), v(10, 32, 128), v(10, 32, 128), v(10, 32, 128),
             v(32, 128), v(3, 32, 128), v(2, 8, 32, 128), v(2, 3, 32, 128), v(4, 64, 128), v(4, 2, 8, 128),
             v(16, 32, 128), v(16, 32, 128), v(16, 32, 128), v(16, 32, 128),
-            v(8, 32, 128), v(8, 32, 128), v(8, 32, 128), v(8, 32, 128), v(8, 32, 128), v(8, 16, 128),
+            v(8, 32, 128), v(8, 32, 128), v(8, 32, 128), v(8, 32, 128), v(8, 32, 128), v(32, 16, 128),
             v(64, 16, 128), v(2, 64, 128), v(8, 128), v(8, 128),
             v(16, 8, 128), v(16, 8, 128), v(8, 8, 128), v(16, 8, 128), v(17, 8, 128),
-            v(4, 64), pltpu.VMEM((1, 128), jnp.int32), v(1, 128), v(1, 128), pltpu.SMEM((64,), jnp.int32),
-            dma((10,)), dma((4,)), dma((5, 8)), dma((5, 8)), dma((2,)), dma((2,)),
+            pltpu.VMEM((384, 128), jnp.bfloat16), v(4, 64), pltpu.VMEM((1, 128), jnp.int32), v(1, 128), v(1, 128), pltpu.SMEM((64,), jnp.int32),
+            dma((10,)), dma((1,)), dma((5, 8)), dma((5, 8)), dma((2,)), dma((2,)),
             dma((16,)), dma((16,)), dma((8,)), dma((8,)), dma((16,)), dma((16,)),
         ],
         compiler_params=pltpu.CompilerParams(collective_id=0, has_side_effects=True),

time: 52.9 us -> 50.5 us (0.955)
  Pallas kernels: 49.7 us -> 47.2 us
    pallas_call x1, Pallas kernels: 49.7 us -> 47.2 us  [local(): pl.pallas_call(kernel, out_shape=(jax.ShapeDtypeStruct(state.shape, F32),...]
where the time goes in v3:
time: 50.5 us; the launch traced here: 50.3 us
  Pallas kernels  47.2 us (93%)
  local copies, waits for them, and re-layouts  2.45 us (5%)
  between operations  0.65 us (1%)
    pallas_call x1, Pallas kernels, local(): pl.pallas_call(kernel, out_shape=(jax.ShapeDtypeStruct(state.shape, F32),...  47.2 us
    unnamed x4, local copies, waits for them, and re-layouts  2.45 us

profile of v3, /device:TPU:1, one launch (start us, length us, event | category | flops | bytes accessed | tf_op | source)
XLA Modules:
  0.0 50.3 jit_solution(12456657201255936377)
XLA Ops:
  0.6 47.2 %shard_map.113 = (f32[64,16,128]{2,1,0:T(8,128)}, f32[4,64]{1,0:T(4,128)}) custom-call(s32[64]{0:T(128)} %mode_in.1, f32[64,16,128]{2,1,0:T(8,128)} %state.1, f32[16,128]{1,0:T(8,128)} %u_vel.1, f32[16,128]{1,0:T(8,128)} %v_vel.1, s32[16,128]{1,0:T(8,128)} %land.1, f32[8,16,128]{2,1,0:T(8,128)} %forcing.1, f32[4,64]{1,0:T(4,128)} %bitcast.5, ...), custom_call_target="tpu_custom_call" | custom-call | tf_op jit(solution)/shard_map/pallas_call | solution.py:476
  47.9 0.0 copy-start
  47.9 1.9 %copy.14 = f32[64,16,128]{2,1,0:T(8,128)} copy(f32[64,16,128]{2,1,0:T(8,128)} %get-tuple-element.8) | data formatting | bytes 1048576
  49.8 0.0 copy-done
  49.8 0.6 %copy.15 = f32[64,4]{0,1:T(4,128)} copy(f32[64,4]{0,1:T(4,128)S(1)} %bitcast.6) | data formatting | bytes 2048
Async XLA Ops:
  47.9 1.9 %copy-start = (f32[4,64]{1,0:T(4,128)S(1)}, f32[4,64]{1,0:T(4,128)}, u32[]{:S(2)}) copy-start(f32[4,64]{1,0:T(4,128)} %get-tuple-element.5) | copy-start | bytes 3076

commit v4 on v3

--- a/solution.py
+++ b/solution.py
@@ -80,11 +80,11 @@
 
 def kernel(
     mode_in, state, u_vel, v_vel, land, forcing, theta, obs_index, obs_values, obs_sigma,
-    fin_out, theta_out,
+    fin, sums, thetas,
     qx, ex, landb, rv, lv, rvr, lvr, mask, tabs, ftab, stabs, coefs, pcoefs,
-    qs, lqs, es, fos, qp, qps, lqps, eps, fops, endp, fin, oall, thx, thr,
-    gp, rs, zs, ag, mat,
-    pick, thl, oix, ova, osg, mode, lsem, osem, hs, hr, xs, xr, rss, rsr, zss, zsr, ags, agr,
+    qs, lqs, es, fos, qp, qps, lqps, eps, fops, endp, oall, thx, thr,
+    gp, rs, zs, ag,
+    pick, thl, oix, ova, osg, mode, lsem, hs, hr, xs, xr, rss, rsr, zss, zsr, ags, agr,
 ):
     z, g, e = lax.axis_index("gx"), lax.axis_index("gy"), lax.axis_index("ens")
     nz, ng = 8, 16
@@ -265,8 +265,6 @@
     slot16 = lane % 32 < 16
     edge = (lane < W) | (lane >= 128 - W)
 
-    out_copy = pltpu.make_async_copy(fin, fin_out, osem.at[0])
-
     def chunk(c, carry):
         m0 = 16 * c
         for copy, _, gets in halo(c, qx, m0, 2 * c):
@@ -323,7 +321,6 @@
             for k in range(4):
                 p = 16 * c + 8 * n + 2 * k + odd
                 fin[p] = jnp.where(edge, pltpu.roll(ends, (112 - 32 * k) % 128, 1), fin[p])
-    out_copy.start()
     for c in range(4):
         x = fin[16 * c : 16 * c + 16].reshape(256, 128)
         part, parts = x, []
@@ -388,15 +385,37 @@
     for c in ag_out:
         c.start()
 
-    th_all = thx[...] + thr[...]
+    thetas[...] = thx[...] + thr[...]
+    for c in ag_in:
+        c.wait_recv()
+    sums[...] = ag[...]
+
+    for copy, sends, _ in halo(4, ex, 0, 8):
+        when(sends, copy.wait_send)
+
+    def drain(c, carry):
+        for copy, sends, _ in halo(c, qx, 16 * c, 2 * c):
+            when(sends, copy.wait_send)
+        return carry
+
+    lax.fori_loop(0, 4, drain, 0)
+    swap_theta.wait_send()
+    swap_seen.wait_send()
+    for c in rs_out + z_out + ag_out:
+        c.wait_send()
+
+
+def solve(fin, sums, thetas, fin_out, theta_out, mat, sem):
+    e = lax.axis_index("ens")
+    out_copy = pltpu.make_async_copy(fin, fin_out, sem)
+    out_copy.start()
+    th_all = thetas[...]
     th_mean = jnp.sum(th_all, axis=1, keepdims=True) * (1.0 / 128.0)
     mat[16] = th_all - th_mean
-    for c in ag_in:
-        c.wait_recv()
-
-    crow = ag[15, 7:8, :]
+    crow = sums[15, 7:8, :]
     sub, ln = iota((8, 128), 0), iota((8, 128), 1)
-    tiles = [ag[t] for t in range(16)]
+    last = sub == 7
+    tiles = [sums[t] for t in range(16)]
     tiles[15] = jnp.where(last, 0.0, tiles[15])
     total = tiles[0]
     for t in range(1, 16):
@@ -453,45 +472,42 @@
     def _():
         theta_out[...] = fresh[0:4, 64:128]
 
-    for copy, sends, _ in halo(4, ex, 0, 8):
-        when(sends, copy.wait_send)
-
-    def drain(c, carry):
-        for copy, sends, _ in halo(c, qx, 16 * c, 2 * c):
-            when(sends, copy.wait_send)
-        return carry
-
-    lax.fori_loop(0, 4, drain, 0)
     out_copy.wait()
-    swap_theta.wait_send()
-    swap_seen.wait_send()
-    for c in rs_out + z_out + ag_out:
-        c.wait_send()
-
-
-def local(state, u_vel, v_vel, land, forcing, member_mode, theta, obs_index, obs_values, obs_sigma):
+
+
+def local(state, u_vel, v_vel, land, forcing, member_mode, theta, *obs):
+    args = (member_mode, state, u_vel, v_vel, land, forcing, theta, *obs)
     hbm = pl.BlockSpec(memory_space=pl.ANY)
     vmem = pl.BlockSpec(memory_space=pltpu.VMEM)
     dma, v = pltpu.SemaphoreType.DMA, lambda *s: pltpu.VMEM(s, F32)
-    return pl.pallas_call(
+    shape = jax.ShapeDtypeStruct
+    fin, sums, thetas = pl.pallas_call(
         kernel,
-        out_shape=(jax.ShapeDtypeStruct(state.shape, F32), jax.ShapeDtypeStruct(theta.shape, F32)),
-        in_specs=[hbm] * 10,
-        out_specs=(hbm, vmem),
+        out_shape=(shape(state.shape, F32), shape((16, 8, 128), F32), shape((8, 128), F32)),
+        in_specs=[pl.BlockSpec(memory_space=pltpu.HBM)] * 10,
+        out_specs=(vmem, vmem, vmem),
         scratch_shapes=[
             v(64, 32, 128), v(16, 32, 128), pltpu.VMEM((16, 128), jnp.int32),
             v(10, 32, 128), v(10, 32, 128), v(10, 32, 128), v(10, 32, 128),
             v(32, 128), v(3, 32, 128), v(2, 8, 32, 128), v(2, 3, 32, 128), v(4, 64, 128), v(4, 2, 8, 128),
             v(16, 32, 128), v(16, 32, 128), v(16, 32, 128), v(16, 32, 128),
             v(8, 32, 128), v(8, 32, 128), v(8, 32, 128), v(8, 32, 128), v(8, 32, 128), v(32, 16, 128),
-            v(64, 16, 128), v(2, 64, 128), v(8, 128), v(8, 128),
-            v(16, 8, 128), v(16, 8, 128), v(8, 8, 128), v(16, 8, 128), v(17, 8, 128),
+            v(2, 64, 128), v(8, 128), v(8, 128),
+            v(16, 8, 128), v(16, 8, 128), v(8, 8, 128), v(16, 8, 128),
             pltpu.VMEM((384, 128), jnp.bfloat16), v(4, 64), pltpu.VMEM((1, 128), jnp.int32), v(1, 128), v(1, 128), pltpu.SMEM((64,), jnp.int32),
-            dma((10,)), dma((1,)), dma((5, 8)), dma((5, 8)), dma((2,)), dma((2,)),
+            dma((10,)), dma((5, 8)), dma((5, 8)), dma((2,)), dma((2,)),
             dma((16,)), dma((16,)), dma((8,)), dma((8,)), dma((16,)), dma((16,)),
         ],
-        compiler_params=pltpu.CompilerParams(collective_id=0, has_side_effects=True),
-    )(member_mode, state, u_vel, v_vel, land, forcing, theta, obs_index, obs_values, obs_sigma)
+        compiler_params=pltpu.CompilerParams(collective_id=0, has_side_effects=True, vmem_limit_bytes=20 * 2**20),
+    )(*[pltpu.with_memory_space_constraint(a, pltpu.HBM) for a in args])
+    return pl.pallas_call(
+        solve,
+        out_shape=(shape(state.shape, F32), shape(theta.shape, F32)),
+        in_specs=[hbm, vmem, vmem],
+        out_specs=(hbm, vmem),
+        scratch_shapes=[v(17, 8, 128), dma(())],
+        compiler_params=pltpu.CompilerParams(vmem_limit_bytes=8 * 2**20),
+    )(fin, sums, thetas)
 
 
 def solution(mesh):

time: 50.5 us -> 48.3 us (0.956)
  local copies, waits for them, and re-layouts: 2.45 us -> 0 us
    unnamed x4 -> x0, local copies, waits for them, and re-layouts: 2.45 us -> none
    pallas_call x1 -> x2, Pallas kernels: 47.2 us -> 47.6 us  [the longest x1 43.2 us: local(): pl.pallas_call(kernel, out_shape=(shape(state.shape, F32), shape((16, 8,...]
where the time goes in v4:
time: 48.3 us; the launch traced here: 48.2 us
  Pallas kernels  47.6 us (99%)
  between operations  0.64 us (1%)
    pallas_call x1, Pallas kernels, local(): pl.pallas_call(kernel, out_shape=(shape(state.shape, F32), shape((16, 8,...  43.2 us
    pallas_call x1, Pallas kernels, local(): pl.pallas_call(solve, out_shape=(shape(state.shape, F32), shape(theta.sha...  4.42 us

profile of v4, /device:TPU:1, one launch (start us, length us, event | category | flops | bytes accessed | tf_op | source)
XLA Modules:
  0.0 48.2 jit_solution(13293602107799679281)
XLA Ops:
  0.6 43.2 %shard_map.113 = (f32[64,16,128]{2,1,0:T(8,128)S(1)}, f32[16,8,128]{2,1,0:T(8,128)S(1)}, f32[8,128]{1,0:T(8,128)S(1)}) custom-call(s32[64]{0:T(128)} %mode_in.1, f32[64,16,128]{2,1,0:T(8,128)} %state.1, f32[16,128]{1,0:T(8,128)} %u_vel.1, f32[16,128]{1,0:T(8,128)} %v_vel.1, s32[16,128]{1,0:T(8,128)} %land.1, f32[8,16,128]{2,1,0:T(8,128)} %forcing.1, ...), custom_call_target="tpu_custom_call" | custom-call | tf_op jit(solution)/shard_map/pallas_call | solution.py:484
  43.8 4.4 %shard_map.114 = (f32[64,16,128]{2,1,0:T(8,128)}, f32[4,64]{1,0:T(4,128)}) custom-call(f32[64,16,128]{2,1,0:T(8,128)S(1)} %get-tuple-element.7.fin, f32[16,8,128]{2,1,0:T(8,128)S(1)} %get-tuple-element.8.sums, f32[8,128]{1,0:T(8,128)S(1)} %get-tuple-element.9.thetas), custom_call_target="tpu_custom_call" | custom-call | tf_op jit(solution)/shard_map/pallas_call | solution.py:503

commit v5 on v4

--- a/solution.py
+++ b/solution.py
@@ -10,7 +10,6 @@
 MESH = pl.DeviceIdType.MESH
 F32 = jnp.float32
 HIGHEST = lax.Precision.HIGHEST
-AHEAD = 4
 
 
 def iota(shape, dim):
@@ -82,9 +81,9 @@
     mode_in, state, u_vel, v_vel, land, forcing, theta, obs_index, obs_values, obs_sigma,
     fin, sums, thetas,
     qx, ex, landb, rv, lv, rvr, lvr, mask, tabs, ftab, stabs, coefs, pcoefs,
-    qs, lqs, es, fos, qp, qps, lqps, eps, fops, endp, oall, thx, thr,
+    qs, lqs, es, fos, qp, endp, oall, thx, thr,
     gp, rs, zs, ag,
-    pick, thl, oix, ova, osg, mode, lsem, hs, hr, xs, xr, rss, rsr, zss, zsr, ags, agr,
+    pick, thl, oix, ova, osg, mode, ysem, zsem, lsem, hs, hr, xs, xr, rss, rsr, zss, zsr, ags, agr,
 ):
     z, g, e = lax.axis_index("gx"), lax.axis_index("gy"), lax.axis_index("ens")
     nz, ng = 8, 16
@@ -100,8 +99,10 @@
         return {"gx": z, "gy": j, "ens": lax.rem(j // 8 + near, 2)}
 
     barrier = pltpu.get_barrier_semaphore()
-    partners = [tile_holder(lax.rem(g + d, ng)) for d in range(1, ng)] + [dev(d, 0) for d in range(1, nz)] + [pair]
-    partners += [dev(a, b) for a in (-1, 0, 1) for b in (-1, 1)]
+    def along_y(d):
+        return tile_holder(lax.rem(g + d + ng, ng))
+
+    partners = [dev(a, b) for a in (-1, 0, 1) for b in (-1, 1)] + [dev(-1, 0), dev(1, 0), pair, along_y(-1), along_y(1)]
     for where in partners:
         pl.semaphore_signal(barrier, inc=1, device_id=where, device_id_type=MESH)
 
@@ -133,7 +134,7 @@
 
     top, bottom, low, high = pl.ds(W, W), pl.ds(16, W), pl.ds(0, W), pl.ds(W + 16, W)
 
-    def halo(c, planes, first, group):
+    def halo(c, planes, first, group, rows):
         at, ga = pl.ds(first, 16), pl.ds(group, 2)
         plan = [
             (planes, at, top, planes, high, (0, -1), up_ok, down_ok),
@@ -146,7 +147,8 @@
             (lv, ga, top, lvr, high, (-1, -1), up_ok, down_ok),
         ]
         out = []
-        for i, (src, a, sr, dst, dr, where, sends, gets) in enumerate(plan):
+        for i in range(2) if rows else range(2, 8):
+            src, a, sr, dst, dr, where, sends, gets = plan[i]
             copy = pltpu.make_async_remote_copy(
                 src_ref=src.at[a, sr, :], dst_ref=dst.at[a, dr, :],
                 send_sem=hs.at[c, i], recv_sem=hr.at[c, i],
@@ -170,6 +172,33 @@
     ex[10, W : W + 16, :] = (1 - landb[...]).astype(F32)
     ex[11:16, W : W + 16, :] = jnp.zeros((5, 16, 128), F32)
     loads[0].wait()
+    pl.semaphore_wait(barrier, len(partners))
+    extra = (4, ex, 0, 8)
+
+    def pass_word(step, along_z):
+        far = 2**step
+        for d in (-far, far):
+            pl.semaphore_signal(ysem.at[step], inc=1, device_id=along_y(d), device_id_type=MESH)
+            if along_z:
+                pl.semaphore_signal(zsem.at[step], inc=1, device_id=dev(d, 0), device_id_type=MESH)
+
+    def hear_word(step, along_z):
+        pl.semaphore_wait(ysem.at[step], 2)
+        if along_z:
+            pl.semaphore_wait(zsem.at[step], 2)
+
+    pass_word(0, True)
+
+    def member_chunk(c):
+        return c, qx, 16 * c, 2 * c
+
+    send(halo(*extra, True))
+
+    def send_rows(c, carry):
+        send(halo(*member_chunk(c), True))
+        return carry
+
+    lax.fori_loop(0, 4, send_rows, 0)
     pack_edges(ex, 0, (W, W + 16), 2, rv, lv, 8)
 
     def pack_own(c, carry):
@@ -177,14 +206,13 @@
         return carry
 
     lax.fori_loop(0, 4, pack_own, 0)
-    pl.semaphore_wait(barrier, len(partners))
-    send(halo(4, ex, 0, 8))
-
-    def send_chunk(c, carry):
-        send(halo(c, qx, 16 * c, 2 * c))
-        return carry
-
-    lax.fori_loop(0, AHEAD, send_chunk, 0)
+    send(halo(*extra, False))
+
+    def send_edges(c, carry):
+        send(halo(*member_chunk(c), False))
+        return carry
+
+    lax.fori_loop(0, 4, send_edges, 0)
 
     for c in loads[5:]:
         c.wait()
@@ -229,15 +257,59 @@
     )
     swap_theta.start()
 
-    for copy, _, gets in halo(4, ex, 0, 8):
-        when(gets, copy.wait_recv)
-    for rows in ((0, W), (W + 16, 32)):
-        pack_edges(ex, 0, rows, 2, rv, lv, 8)
+    def wait_for(copies):
+        for copy, _, gets in copies:
+            when(gets, copy.wait_recv)
+
+    site = oix[...]
+    col_pick = jnp.broadcast_to(site % 128, (128, 128)) == iota((128, 128), 0)
+    for n in range(3):
+        pick[128 * n : 128 * n + 128, :] = col_pick.astype(F32).astype(jnp.bfloat16)
+    site_row = jnp.broadcast_to(site // 128, (16, 128)) == iota((16, 128), 0)
+    lane = iota((16, 128), 1)
+    slot16 = lane % 32 < 16
+    edge = (lane < W) | (lane >= 128 - W)
+    slot32 = iota((32, 128), 1) // 32
+
+    wait_for(halo(*extra, True))
+    hear_word(0, True)
+    pass_word(1, True)
     o = ex[10]
     tabs[0] = o
     tabs[1] = 0.5 * ex[8] * o
     tabs[2] = 0.5 * ex[9] * o
-    slot32 = iota((32, 128), 1) // 32
+
+    def chunk(c, carry):
+        m0 = 16 * c
+        wait_for(halo(*member_chunk(c), True))
+        for p in range(16):
+            fos[p] = coefs[3, pl.ds(m0 + p, 1), :] * ex[mode[m0 + p]]
+
+        def keep(p, new):
+            fin[m0 + p] = new
+
+        advance(
+            lambda p, a, n: qx[m0 + p, a : a + n, :], 16,
+            [lambda p, t=t: coefs[t, pl.ds(m0 + p, 1), :] for t in range(3)],
+            [lambda p, a, n, t=t: tabs[t, a : a + n, :] for t in range(3)],
+            lambda p, a, n: fos[p, a : a + n, :], qs, lqs, es, mask, keep,
+        )
+        return carry
+
+    lax.fori_loop(0, 4, chunk, 0)
+
+    hear_word(1, True)
+    pass_word(2, False)
+    for rows in ((0, W), (W + 16, 32)):
+        pack_edges(ex, 0, rows, 2, rv, lv, 8)
+
+    def pack_halo(c, carry):
+        for rows in ((0, W), (W + 16, 32)):
+            pack_edges(qx, 16 * c, rows, 2, rv, lv, 2 * c)
+        return carry
+
+    lax.fori_loop(0, 4, pack_halo, 0)
+    wait_for(halo(*extra, False))
 
     def spread(x, k):
         y = jnp.where(slot32 == k, x, 0.0)
@@ -256,40 +328,15 @@
         stabs[side, 1] = 0.5 * spread(even, 0) * o
         stabs[side, 2] = 0.5 * spread(odd, 0) * o
 
-    site = oix[...]
-    col_pick = jnp.broadcast_to(site % 128, (128, 128)) == iota((128, 128), 0)
-    for n in range(3):
-        pick[128 * n : 128 * n + 128, :] = col_pick.astype(F32).astype(jnp.bfloat16)
-    site_row = jnp.broadcast_to(site // 128, (16, 128)) == iota((16, 128), 0)
-    lane = iota((16, 128), 1)
-    slot16 = lane % 32 < 16
-    edge = (lane < W) | (lane >= 128 - W)
-
-    def chunk(c, carry):
-        m0 = 16 * c
-        for copy, _, gets in halo(c, qx, m0, 2 * c):
-            when(gets, copy.wait_recv)
-
-        @pl.when(c + AHEAD < 4)
-        def _():
-            send_chunk(c + AHEAD, 0)
-
-        for rows in ((0, W), (W + 16, 32)):
-            pack_edges(qx, m0, rows, 2, rv, lv, 2 * c)
-        for p in range(16):
-            fos[p] = coefs[3, pl.ds(m0 + p, 1), :] * ex[mode[m0 + p]]
-
-        def keep(p, new):
-            fin[m0 + p] = new
-
-        advance(
-            lambda p, a, n: qx[m0 + p, a : a + n, :], 16,
-            [lambda p, t=t: coefs[t, pl.ds(m0 + p, 1), :] for t in range(3)],
-            [lambda p, a, n, t=t: tabs[t, a : a + n, :] for t in range(3)],
-            lambda p, a, n: fos[p, a : a + n, :], qs, lqs, es, mask, keep,
-        )
-        for n in range(2):
-            gr = 2 * c + n
+    def edges_here(c, carry):
+        wait_for(halo(*member_chunk(c), False))
+        return carry
+
+    lax.fori_loop(0, 4, edges_here, 0)
+
+    def strips(c, carry):
+        for n in range(4):
+            gr = 4 * c + n
             both = strips_of(rv[gr], lv[gr], rvr[gr], lvr[gr], 0, 32)
             for side in range(2):
                 for odd in range(2):
@@ -297,22 +344,22 @@
                     qp[p] = both[side][odd]
                     f = None
                     for k in range(4):
-                        x = ftab[side, mode[m0 + 8 * n + 2 * k + odd]]
+                        x = ftab[side, mode[8 * gr + 2 * k + odd]]
                         f = x if f is None else jnp.where(slot32 == k, x, f)
-                    fops[p] = pcoefs[3, odd, pl.ds(gr, 1), :] * f
-
-        def keep_strip(p, new):
-            endp[8 * c + p] = new
+                    fos[p] = pcoefs[3, odd, pl.ds(gr, 1), :] * f
+
+        def keep(p, new):
+            endp[16 * c + p] = new
 
         advance(
-            lambda p, a, n: qp[p, a : a + n, :], 8,
-            [lambda p, t=t: pcoefs[t, p % 2, pl.ds(2 * c + p // 4, 1), :] for t in range(3)],
+            lambda p, a, n: qp[p, a : a + n, :], 16,
+            [lambda p, t=t: pcoefs[t, p % 2, pl.ds(4 * c + p // 4, 1), :] for t in range(3)],
             [lambda p, a, n, t=t: stabs[(p // 2) % 2, t, a : a + n, :] for t in range(3)],
-            lambda p, a, n: fops[p, a : a + n, :], qps, lqps, eps, mask, keep_strip,
+            lambda p, a, n: fos[p, a : a + n, :], qs, lqs, es, mask, keep,
         )
         return carry
 
-    lax.fori_loop(0, 4, chunk, 0)
+    lax.fori_loop(0, 2, strips, 0)
 
     for c in range(4):
         for q in range(4):
@@ -368,6 +415,7 @@
                 device_id=where, device_id_type=MESH))
         return outs, ins
 
+    hear_word(2, False)
     rs[g] = gp[g]
     rs_out, rs_in = spread_out(lambda j: gp.at[j], rs, rss, rsr, ng, g, tile_holder)
     for c in rs_out:
@@ -390,15 +438,19 @@
         c.wait_recv()
     sums[...] = ag[...]
 
-    for copy, sends, _ in halo(4, ex, 0, 8):
-        when(sends, copy.wait_send)
-
-    def drain(c, carry):
-        for copy, sends, _ in halo(c, qx, 16 * c, 2 * c):
+    def drain(copies):
+        for copy, sends, _ in copies:
             when(sends, copy.wait_send)
-        return carry
-
-    lax.fori_loop(0, 4, drain, 0)
+
+    drain(halo(*extra, True))
+    drain(halo(*extra, False))
+
+    def drain_chunk(c, carry):
+        drain(halo(*member_chunk(c), True))
+        drain(halo(*member_chunk(c), False))
+        return carry
+
+    lax.fori_loop(0, 4, drain_chunk, 0)
     swap_theta.wait_send()
     swap_seen.wait_send()
     for c in rs_out + z_out + ag_out:
@@ -491,11 +543,11 @@
             v(10, 32, 128), v(10, 32, 128), v(10, 32, 128), v(10, 32, 128),
             v(32, 128), v(3, 32, 128), v(2, 8, 32, 128), v(2, 3, 32, 128), v(4, 64, 128), v(4, 2, 8, 128),
             v(16, 32, 128), v(16, 32, 128), v(16, 32, 128), v(16, 32, 128),
-            v(8, 32, 128), v(8, 32, 128), v(8, 32, 128), v(8, 32, 128), v(8, 32, 128), v(32, 16, 128),
+            v(16, 32, 128), v(32, 16, 128),
             v(2, 64, 128), v(8, 128), v(8, 128),
             v(16, 8, 128), v(16, 8, 128), v(8, 8, 128), v(16, 8, 128),
             pltpu.VMEM((384, 128), jnp.bfloat16), v(4, 64), pltpu.VMEM((1, 128), jnp.int32), v(1, 128), v(1, 128), pltpu.SMEM((64,), jnp.int32),
-            dma((10,)), dma((5, 8)), dma((5, 8)), dma((2,)), dma((2,)),
+            pltpu.SemaphoreType.REGULAR((3,)), pltpu.SemaphoreType.REGULAR((2,)), dma((10,)), dma((5, 8)), dma((5, 8)), dma((2,)), dma((2,)),
             dma((16,)), dma((16,)), dma((8,)), dma((8,)), dma((16,)), dma((16,)),
         ],
         compiler_params=pltpu.CompilerParams(collective_id=0, has_side_effects=True, vmem_limit_bytes=20 * 2**20),

time: 48.3 us -> 46.4 us (0.961)
  Pallas kernels: 47.6 us -> 45.7 us
    pallas_call x1, Pallas kernels: 43.2 us -> 41.2 us  [local(): pl.pallas_call(kernel, out_shape=(shape(state.shape, F32), shape((16, 8,...]
where the time goes in v5:
time: 46.4 us; the launch traced here: 46.3 us
  Pallas kernels  45.7 us (98%)
  between operations  0.64 us (1%)
    pallas_call x1, Pallas kernels, local(): pl.pallas_call(kernel, out_shape=(shape(state.shape, F32), shape((16, 8,...  41.2 us
    pallas_call x1, Pallas kernels, local(): pl.pallas_call(solve, out_shape=(shape(state.shape, F32), shape(theta.sha...  4.42 us

profile of v5, /device:TPU:1, one launch (start us, length us, event | category | flops | bytes accessed | tf_op | source)
XLA Modules:
  0.0 46.3 jit_solution(15956086799749903331)
XLA Ops:
  0.6 41.2 %shard_map.113 = (f32[64,16,128]{2,1,0:T(8,128)S(1)}, f32[16,8,128]{2,1,0:T(8,128)S(1)}, f32[8,128]{1,0:T(8,128)S(1)}) custom-call(s32[64]{0:T(128)} %mode_in.1, f32[64,16,128]{2,1,0:T(8,128)} %state.1, f32[16,128]{1,0:T(8,128)} %u_vel.1, f32[16,128]{1,0:T(8,128)} %v_vel.1, s32[16,128]{1,0:T(8,128)} %land.1, f32[8,16,128]{2,1,0:T(8,128)} %forcing.1, ...), custom_call_target="tpu_custom_call" | custom-call | tf_op jit(solution)/shard_map/pallas_call | solution.py:536
  41.9 4.4 %shard_map.114 = (f32[64,16,128]{2,1,0:T(8,128)}, f32[4,64]{1,0:T(4,128)}) custom-call(f32[64,16,128]{2,1,0:T(8,128)S(1)} %get-tuple-element.7.fin, f32[16,8,128]{2,1,0:T(8,128)S(1)} %get-tuple-element.8.sums, f32[8,128]{1,0:T(8,128)S(1)} %get-tuple-element.9.thetas), custom_call_target="tpu_custom_call" | custom-call | tf_op jit(solution)/shard_map/pallas_call | solution.py:555

commit v6 on v5

--- a/solution.py
+++ b/solution.py
@@ -398,45 +398,54 @@
     dims = (((1,), (1,)), ((), ()))
     gram = lax.dot_general(anomaly, anomaly, dims, precision=HIGHEST, preferred_element_type=F32)
     cvec = lax.dot_general(miss, anomaly, dims, precision=HIGHEST, preferred_element_type=F32)
-    gp[...] = gram.reshape(16, 8, 128)
-    last = iota((8, 128), 0) == 7
-    gp[15] = jnp.where(last, cvec, gram[120:128])
-
-    def spread_out(src, dst, ssem, rsem, count, me, place):
-        outs, ins = [], []
-        for d in range(1, count):
-            j = lax.rem(me + d, count)
-            where = place(j)
-            outs.append(pltpu.make_async_remote_copy(
-                src_ref=src(j), dst_ref=dst.at[me], send_sem=ssem.at[d], recv_sem=rsem.at[me],
-                device_id=where, device_id_type=MESH))
-            ins.append(pltpu.make_async_remote_copy(
-                src_ref=src(j), dst_ref=dst.at[j], send_sem=ssem.at[d], recv_sem=rsem.at[j],
-                device_id=where, device_id_type=MESH))
-        return outs, ins
+    last = iota((128, 128), 0) == 127
+    gp[...] = jnp.where(last, cvec[0:1, :], gram).reshape(8, 16, 128)
+
+    owner, mine = lax.rem(g, 2) == 1, g // 2
+
+    def to(src, dst, ssem, rsem, where):
+        return pltpu.make_async_remote_copy(
+            src_ref=src, dst_ref=dst, send_sem=ssem, recv_sem=rsem, device_id=where, device_id_type=MESH
+        )
+
+    def rows_to_owner(d):
+        j = lax.rem(mine + d, 8)
+        return to(gp.at[j], rs.at[g], rss.at[d], rsr.at[g], tile_holder(2 * j + 1))
+
+    def rows_to_gx(d):
+        where = {"gx": lax.rem(z + d, nz), "gy": g, "ens": e}
+        return to(zs.at[z], zs.at[z], zss.at[d], zsr.at[z], where)
+
+    def rows_to_all(d):
+        return to(ag.at[mine], ag.at[mine], ags.at[d], agr.at[mine], tile_holder(lax.rem(g + d, ng)))
+
+    def arrived(ref, i, rsem, ssem):
+        to(ref.at[i], ref.at[i], ssem, rsem.at[i], pair).wait_recv()
 
     hear_word(2, False)
-    rs[g] = gp[g]
-    rs_out, rs_in = spread_out(lambda j: gp.at[j], rs, rss, rsr, ng, g, tile_holder)
-    for c in rs_out:
-        c.start()
-    for c in rs_in:
-        c.wait_recv()
-    zs[z] = jnp.sum(rs[...], axis=0)
-    z_out, z_in = spread_out(lambda j: zs.at[z], zs, zss, zsr, nz, z, lambda j: {"gx": j, "gy": g, "ens": e})
-    for c in z_out:
-        c.start()
-    for c in z_in:
-        c.wait_recv()
-    ag[g] = jnp.sum(zs[...], axis=0)
-    ag_out, ag_in = spread_out(lambda j: ag.at[g], ag, ags, agr, ng, g, tile_holder)
-    for c in ag_out:
-        c.start()
+    for d in range(1, 8):
+        rows_to_owner(d).start()
+    pl.when(jnp.logical_not(owner))(lambda: rows_to_owner(0).start())
+
+    @pl.when(owner)
+    def _():
+        rs[g] = gp[mine]
+        for d in range(1, ng):
+            arrived(rs, lax.rem(g + d, ng), rsr, rss.at[0])
+        zs[z] = jnp.sum(rs[...], axis=0)
+        for d in range(1, nz):
+            rows_to_gx(d).start()
+        for d in range(1, nz):
+            arrived(zs, lax.rem(z + d, nz), zsr, zss.at[0])
+        ag[mine] = jnp.sum(zs[...], axis=0)
+        for d in range(1, ng):
+            rows_to_all(d).start()
 
     thetas[...] = thx[...] + thr[...]
-    for c in ag_in:
-        c.wait_recv()
-    sums[...] = ag[...]
+    for d in range(1, 8):
+        arrived(ag, lax.rem(mine + d, 8), agr, ags.at[0])
+    pl.when(jnp.logical_not(owner))(lambda: arrived(ag, mine, agr, ags.at[0]))
+    sums[...] = ag[...].reshape(16, 8, 128)
 
     def drain(copies):
         for copy, sends, _ in copies:
@@ -453,8 +462,16 @@
     lax.fori_loop(0, 4, drain_chunk, 0)
     swap_theta.wait_send()
     swap_seen.wait_send()
-    for c in rs_out + z_out + ag_out:
-        c.wait_send()
+    for d in range(1, 8):
+        rows_to_owner(d).wait_send()
+    pl.when(jnp.logical_not(owner))(lambda: rows_to_owner(0).wait_send())
+
+    @pl.when(owner)
+    def _():
+        for d in range(1, nz):
+            rows_to_gx(d).wait_send()
+        for d in range(1, ng):
+            rows_to_all(d).wait_send()
 
 
 def solve(fin, sums, thetas, fin_out, theta_out, mat, sem):
@@ -545,10 +562,10 @@
             v(16, 32, 128), v(16, 32, 128), v(16, 32, 128), v(16, 32, 128),
             v(16, 32, 128), v(32, 16, 128),
             v(2, 64, 128), v(8, 128), v(8, 128),
-            v(16, 8, 128), v(16, 8, 128), v(8, 8, 128), v(16, 8, 128),
+            v(8, 16, 128), v(16, 16, 128), v(8, 16, 128), v(8, 16, 128),
             pltpu.VMEM((384, 128), jnp.bfloat16), v(4, 64), pltpu.VMEM((1, 128), jnp.int32), v(1, 128), v(1, 128), pltpu.SMEM((64,), jnp.int32),
             pltpu.SemaphoreType.REGULAR((3,)), pltpu.SemaphoreType.REGULAR((2,)), dma((10,)), dma((5, 8)), dma((5, 8)), dma((2,)), dma((2,)),
-            dma((16,)), dma((16,)), dma((8,)), dma((8,)), dma((16,)), dma((16,)),
+            dma((8,)), dma((16,)), dma((8,)), dma((8,)), dma((16,)), dma((8,)),
         ],
         compiler_params=pltpu.CompilerParams(collective_id=0, has_side_effects=True, vmem_limit_bytes=20 * 2**20),
     )(*[pltpu.with_memory_space_constraint(a, pltpu.HBM) for a in args])

time: 46.4 us -> 45 us (0.970)
  Pallas kernels: 45.7 us -> 44.3 us
    pallas_call x1, Pallas kernels: 41.2 us -> 39.8 us  [local(): pl.pallas_call(kernel, out_shape=(shape(state.shape, F32), shape((16, 8,...]
where the time goes in v6:
time: 45 us; the launch traced here: 44.9 us
  Pallas kernels  44.3 us (98%)
  between operations  0.64 us (1%)
    pallas_call x1, Pallas kernels, local(): pl.pallas_call(kernel, out_shape=(shape(state.shape, F32), shape((16, 8,...  39.8 us
    pallas_call x1, Pallas kernels, local(): pl.pallas_call(solve, out_shape=(shape(state.shape, F32), shape(theta.sha...  4.42 us

profile of v6, /device:TPU:1, one launch (start us, length us, event | category | flops | bytes accessed | tf_op | source)
XLA Modules:
  0.0 44.9 jit_solution(3419880277438537462)
XLA Ops:
  0.6 39.8 %shard_map.113 = (f32[64,16,128]{2,1,0:T(8,128)S(1)}, f32[16,8,128]{2,1,0:T(8,128)S(1)}, f32[8,128]{1,0:T(8,128)S(1)}) custom-call(s32[64]{0:T(128)} %mode_in.1, f32[64,16,128]{2,1,0:T(8,128)} %state.1, f32[16,128]{1,0:T(8,128)} %u_vel.1, f32[16,128]{1,0:T(8,128)} %v_vel.1, s32[16,128]{1,0:T(8,128)} %land.1, f32[8,16,128]{2,1,0:T(8,128)} %forcing.1, ...), custom_call_target="tpu_custom_call" | custom-call | tf_op jit(solution)/shard_map/pallas_call | solution.py:553
  40.5 4.4 %shard_map.114 = (f32[64,16,128]{2,1,0:T(8,128)}, f32[4,64]{1,0:T(4,128)}) custom-call(f32[64,16,128]{2,1,0:T(8,128)S(1)} %get-tuple-element.7.fin, f32[16,8,128]{2,1,0:T(8,128)S(1)} %get-tuple-element.8.sums, f32[8,128]{1,0:T(8,128)S(1)} %get-tuple-element.9.thetas), custom_call_target="tpu_custom_call" | custom-call | tf_op jit(solution)/shard_map/pallas_call | solution.py:572

commit v7 on v6

--- a/solution.py
+++ b/solution.py
@@ -124,18 +124,18 @@
 
     @pl.when(jnp.logical_not(up_ok))
     def _():
-        for ref in (qx, ex, rvr, lvr):
+        for ref in (qx, ex, rv, lv, rvr, lvr):
             ref[:, 0:W, :] = jnp.zeros((ref.shape[0], W, 128), F32)
 
     @pl.when(jnp.logical_not(down_ok))
     def _():
-        for ref in (qx, ex, rvr, lvr):
+        for ref in (qx, ex, rv, lv, rvr, lvr):
             ref[:, W + 16 :, :] = jnp.zeros((ref.shape[0], W, 128), F32)
 
     top, bottom, low, high = pl.ds(W, W), pl.ds(16, W), pl.ds(0, W), pl.ds(W + 16, W)
 
     def halo(c, planes, first, group, rows):
-        at, ga = pl.ds(first, 16), pl.ds(group, 2)
+        at, ga = pl.ds(first, 16 if planes is qx else 11), pl.ds(group, 2)
         plan = [
             (planes, at, top, planes, high, (0, -1), up_ok, down_ok),
             (planes, at, bottom, planes, low, (0, 1), down_ok, up_ok),
@@ -145,9 +145,13 @@
             (rv, ga, top, rvr, high, (1, -1), up_ok, down_ok),
             (lv, ga, bottom, lvr, low, (-1, 1), down_ok, up_ok),
             (lv, ga, top, lvr, high, (-1, -1), up_ok, down_ok),
+            (rv, ga, top, rv, high, (0, -1), up_ok, down_ok),
+            (rv, ga, bottom, rv, low, (0, 1), down_ok, up_ok),
+            (lv, ga, top, lv, high, (0, -1), up_ok, down_ok),
+            (lv, ga, bottom, lv, low, (0, 1), down_ok, up_ok),
         ]
         out = []
-        for i in range(2) if rows else range(2, 8):
+        for i in range(2) if rows else range(2, 12):
             src, a, sr, dst, dr, where, sends, gets = plan[i]
             copy = pltpu.make_async_remote_copy(
                 src_ref=src.at[a, sr, :], dst_ref=dst.at[a, dr, :],
@@ -300,15 +304,6 @@
 
     hear_word(1, True)
     pass_word(2, False)
-    for rows in ((0, W), (W + 16, 32)):
-        pack_edges(ex, 0, rows, 2, rv, lv, 8)
-
-    def pack_halo(c, carry):
-        for rows in ((0, W), (W + 16, 32)):
-            pack_edges(qx, 16 * c, rows, 2, rv, lv, 2 * c)
-        return carry
-
-    lax.fori_loop(0, 4, pack_halo, 0)
     wait_for(halo(*extra, False))
 
     def spread(x, k):
@@ -507,15 +502,18 @@
         piv = mat[k]
         ahead = lanes_of(piv, base + 8) if k < 15 else []
         row = jnp.where(front, jnp.where(ln == sub + base, 1.0, 0.0), piv)
+        scale = jnp.zeros((8, 128), F32)
         for i in range(8):
-            at = [row_of(cols[j], i) for j in range(i, 8)]
-            inv = 1.0 / at[0]
+            inv = 1.0 / row_of(cols[i], i)
             mine = sub == i
-            step = jnp.where(mine, -1.0, cols[i])
-            row = jnp.where(mine, 0.0, row) - step * (row_of(row, i) * inv)
+            step = jnp.where(mine, 0.0, cols[i]) * inv
+            scale = jnp.where(mine, inv, scale)
+            row = row - step * row_of(row, i)
             for j in range(i + 1, 8):
-                cols[j] = jnp.where(mine, 0.0, cols[j]) - step * (at[j - i] * inv)
-            ahead = [jnp.where(mine, 0.0, x) - step * (row_of(x, i) * inv) for x in ahead]
+                cols[j] = cols[j] - step * row_of(cols[j], i)
+            ahead = [x - step * row_of(x, i) for x in ahead]
+        row = row * scale
+        ahead = [x * scale for x in ahead]
         row = jnp.where(front, -row, row)
         rows = [row_of(row, i) for i in range(8)]
         for t in range(k + 1, 17):
@@ -564,7 +562,7 @@
             v(2, 64, 128), v(8, 128), v(8, 128),
             v(8, 16, 128), v(16, 16, 128), v(8, 16, 128), v(8, 16, 128),
             pltpu.VMEM((384, 128), jnp.bfloat16), v(4, 64), pltpu.VMEM((1, 128), jnp.int32), v(1, 128), v(1, 128), pltpu.SMEM((64,), jnp.int32),
-            pltpu.SemaphoreType.REGULAR((3,)), pltpu.SemaphoreType.REGULAR((2,)), dma((10,)), dma((5, 8)), dma((5, 8)), dma((2,)), dma((2,)),
+            pltpu.SemaphoreType.REGULAR((3,)), pltpu.SemaphoreType.REGULAR((2,)), dma((10,)), dma((5, 12)), dma((5, 12)), dma((2,)), dma((2,)),
             dma((8,)), dma((16,)), dma((8,)), dma((8,)), dma((16,)), dma((8,)),
         ],
         compiler_params=pltpu.CompilerParams(collective_id=0, has_side_effects=True, vmem_limit_bytes=20 * 2**20),

time: 45 us -> 44.4 us (0.987)
  Pallas kernels: 44.3 us -> 43.6 us
    pallas_call x1, Pallas kernels: 39.8 us -> 39.4 us  [local(): pl.pallas_call(kernel, out_shape=(shape(state.shape, F32), shape((16, 8,...]
where the time goes in v7:
time: 44.4 us; the launch traced here: 44.3 us
  Pallas kernels  43.6 us (98%)
  between operations  0.64 us (1%)
    pallas_call x1, Pallas kernels, local(): pl.pallas_call(kernel, out_shape=(shape(state.shape, F32), shape((16, 8,...  39.4 us
    pallas_call x1, Pallas kernels, local(): pl.pallas_call(solve, out_shape=(shape(state.shape, F32), shape(theta.sha...  4.25 us

profile of v7, /device:TPU:1, one launch (start us, length us, event | category | flops | bytes accessed | tf_op | source)
XLA Modules:
  0.0 44.3 jit_solution(7231388845117749197)
XLA Ops:
  0.6 39.4 %shard_map.113 = (f32[64,16,128]{2,1,0:T(8,128)S(1)}, f32[16,8,128]{2,1,0:T(8,128)S(1)}, f32[8,128]{1,0:T(8,128)S(1)}) custom-call(s32[64]{0:T(128)} %mode_in.1, f32[64,16,128]{2,1,0:T(8,128)} %state.1, f32[16,128]{1,0:T(8,128)} %u_vel.1, f32[16,128]{1,0:T(8,128)} %v_vel.1, s32[16,128]{1,0:T(8,128)} %land.1, f32[8,16,128]{2,1,0:T(8,128)} %forcing.1, ...), custom_call_target="tpu_custom_call" | custom-call | tf_op jit(solution)/shard_map/pallas_call | solution.py:551
  40.0 4.3 %shard_map.114 = (f32[64,16,128]{2,1,0:T(8,128)}, f32[4,64]{1,0:T(4,128)}) custom-call(f32[64,16,128]{2,1,0:T(8,128)S(1)} %get-tuple-element.7.fin, f32[16,8,128]{2,1,0:T(8,128)S(1)} %get-tuple-element.8.sums, f32[8,128]{1,0:T(8,128)S(1)} %get-tuple-element.9.thetas), custom_call_target="tpu_custom_call" | custom-call | tf_op jit(solution)/shard_map/pallas_call | solution.py:570

commit v8 on v7

--- a/solution.py
+++ b/solution.py
@@ -437,11 +437,6 @@
             rows_to_all(d).start()
 
     thetas[...] = thx[...] + thr[...]
-    for d in range(1, 8):
-        arrived(ag, lax.rem(mine + d, 8), agr, ags.at[0])
-    pl.when(jnp.logical_not(owner))(lambda: arrived(ag, mine, agr, ags.at[0]))
-    sums[...] = ag[...].reshape(16, 8, 128)
-
     def drain(copies):
         for copy, sends, _ in copies:
             when(sends, copy.wait_send)
@@ -465,6 +460,14 @@
     def _():
         for d in range(1, nz):
             rows_to_gx(d).wait_send()
+
+    for d in range(1, 8):
+        arrived(ag, lax.rem(mine + d, 8), agr, ags.at[0])
+    pl.when(jnp.logical_not(owner))(lambda: arrived(ag, mine, agr, ags.at[0]))
+    sums[...] = ag[...].reshape(16, 8, 128)
+
+    @pl.when(owner)
+    def _():
         for d in range(1, ng):
             rows_to_all(d).wait_send()
 

time: 44.4 us -> 44.3 us (level)
  no operation moved by 1% of the time
where the time goes in v8:
time: 44.3 us; the launch traced here: 44.2 us
  Pallas kernels  43.5 us (98%)
  between operations  0.64 us (1%)
    pallas_call x1, Pallas kernels, local(): pl.pallas_call(kernel, out_shape=(shape(state.shape, F32), shape((16, 8,...  39.3 us
    pallas_call x1, Pallas kernels, local(): pl.pallas_call(solve, out_shape=(shape(state.shape, F32), shape(theta.sha...  4.25 us

profile of v8, /device:TPU:1, one launch (start us, length us, event | category | flops | bytes accessed | tf_op | source)
XLA Modules:
  0.0 44.2 jit_solution(14960263557900965406)
XLA Ops:
  0.6 39.3 %shard_map.113 = (f32[64,16,128]{2,1,0:T(8,128)S(1)}, f32[16,8,128]{2,1,0:T(8,128)S(1)}, f32[8,128]{1,0:T(8,128)S(1)}) custom-call(s32[64]{0:T(128)} %mode_in.1, f32[64,16,128]{2,1,0:T(8,128)} %state.1, f32[16,128]{1,0:T(8,128)} %u_vel.1, f32[16,128]{1,0:T(8,128)} %v_vel.1, s32[16,128]{1,0:T(8,128)} %land.1, f32[8,16,128]{2,1,0:T(8,128)} %forcing.1, ...), custom_call_target="tpu_custom_call" | custom-call | tf_op jit(solution)/shard_map/pallas_call | solution.py:554
  39.9 4.3 %shard_map.114 = (f32[64,16,128]{2,1,0:T(8,128)}, f32[4,64]{1,0:T(4,128)}) custom-call(f32[64,16,128]{2,1,0:T(8,128)S(1)} %get-tuple-element.7.fin, f32[16,8,128]{2,1,0:T(8,128)S(1)} %get-tuple-element.8.sums, f32[8,128]{1,0:T(8,128)S(1)} %get-tuple-element.9.thetas), custom_call_target="tpu_custom_call" | custom-call | tf_op jit(solution)/shard_map/pallas_call | solution.py:573

commit v9 on v8

--- a/solution.py
+++ b/solution.py
@@ -330,8 +330,8 @@
     lax.fori_loop(0, 4, edges_here, 0)
 
     def strips(c, carry):
-        for n in range(4):
-            gr = 4 * c + n
+        for n in range(8):
+            gr = 8 * c + n
             both = strips_of(rv[gr], lv[gr], rvr[gr], lvr[gr], 0, 32)
             for side in range(2):
                 for odd in range(2):
@@ -344,17 +344,17 @@
                     fos[p] = pcoefs[3, odd, pl.ds(gr, 1), :] * f
 
         def keep(p, new):
-            endp[16 * c + p] = new
+            endp[32 * c + p] = new
 
         advance(
-            lambda p, a, n: qp[p, a : a + n, :], 16,
-            [lambda p, t=t: pcoefs[t, p % 2, pl.ds(4 * c + p // 4, 1), :] for t in range(3)],
+            lambda p, a, n: qp[p, a : a + n, :], 32,
+            [lambda p, t=t: pcoefs[t, p % 2, pl.ds(8 * c + p // 4, 1), :] for t in range(3)],
             [lambda p, a, n, t=t: stabs[(p // 2) % 2, t, a : a + n, :] for t in range(3)],
             lambda p, a, n: fos[p, a : a + n, :], qs, lqs, es, mask, keep,
         )
         return carry
 
-    lax.fori_loop(0, 2, strips, 0)
+    strips(0, 0)
 
     for c in range(4):
         for q in range(4):
@@ -560,8 +560,8 @@
             v(64, 32, 128), v(16, 32, 128), pltpu.VMEM((16, 128), jnp.int32),
             v(10, 32, 128), v(10, 32, 128), v(10, 32, 128), v(10, 32, 128),
             v(32, 128), v(3, 32, 128), v(2, 8, 32, 128), v(2, 3, 32, 128), v(4, 64, 128), v(4, 2, 8, 128),
-            v(16, 32, 128), v(16, 32, 128), v(16, 32, 128), v(16, 32, 128),
-            v(16, 32, 128), v(32, 16, 128),
+            v(32, 32, 128), v(32, 32, 128), v(32, 32, 128), v(32, 32, 128),
+            v(32, 32, 128), v(32, 16, 128),
             v(2, 64, 128), v(8, 128), v(8, 128),
             v(8, 16, 128), v(16, 16, 128), v(8, 16, 128), v(8, 16, 128),
             pltpu.VMEM((384, 128), jnp.bfloat16), v(4, 64), pltpu.VMEM((1, 128), jnp.int32), v(1, 128), v(1, 128), pltpu.SMEM((64,), jnp.int32),

time: 44.3 us -> 44.1 us (level)
  no operation moved by 1% of the time
where the time goes in v9:
time: 44.1 us; the launch traced here: 44 us
  Pallas kernels  43.4 us (98%)
  between operations  0.64 us (1%)
    pallas_call x1, Pallas kernels, local(): pl.pallas_call(kernel, out_shape=(shape(state.shape, F32), shape((16, 8,...  39.1 us
    pallas_call x1, Pallas kernels, local(): pl.pallas_call(solve, out_shape=(shape(state.shape, F32), shape(theta.sha...  4.25 us

profile of v9, /device:TPU:1, one launch (start us, length us, event | category | flops | bytes accessed | tf_op | source)
XLA Modules:
  0.0 44.0 jit_solution(11486017338844630630)
XLA Ops:
  0.6 39.1 %shard_map.113 = (f32[64,16,128]{2,1,0:T(8,128)S(1)}, f32[16,8,128]{2,1,0:T(8,128)S(1)}, f32[8,128]{1,0:T(8,128)S(1)}) custom-call(s32[64]{0:T(128)} %mode_in.1, f32[64,16,128]{2,1,0:T(8,128)} %state.1, f32[16,128]{1,0:T(8,128)} %u_vel.1, f32[16,128]{1,0:T(8,128)} %v_vel.1, s32[16,128]{1,0:T(8,128)} %land.1, f32[8,16,128]{2,1,0:T(8,128)} %forcing.1, ...), custom_call_target="tpu_custom_call" | custom-call | tf_op jit(solution)/shard_map/pallas_call | solution.py:554
  39.7 4.3 %shard_map.114 = (f32[64,16,128]{2,1,0:T(8,128)}, f32[4,64]{1,0:T(4,128)}) custom-call(f32[64,16,128]{2,1,0:T(8,128)S(1)} %get-tuple-element.7.fin, f32[16,8,128]{2,1,0:T(8,128)S(1)} %get-tuple-element.8.sums, f32[8,128]{1,0:T(8,128)S(1)} %get-tuple-element.9.thetas), custom_call_target="tpu_custom_call" | custom-call | tf_op jit(solution)/shard_map/pallas_call | solution.py:573
